TPU v7x, 32 devices: a whole 2x2x4 slice. The times are simulated.
32 devices in a mesh: rows: 8 (over y, x, core), rep: 4 (over z).
Axes of the slice: x: 2, y: 2, z: 4, core: 2. Of those that a mesh axis runs over, the one named last changes fastest.
Arguments:
- x_tiles: bfloat16 [64, 10, 128, 128], P('rows'), may hold values from -2.5 to 2.5
- giant_tiles: bfloat16 [64, 10, 128, 128], P('rows'), may hold values from -2.5 to 2.5
- coeffs: float32 [3], replicated, may hold values from 0.5 to 1.5
- pattern: int32 [64, 10], replicated, may hold values from 0 to 63, as said below
Outputs:
- squared: bfloat16 [64, 10, 128, 128], P('rows')
- result: bfloat16 [64, 10, 128, 128], P('rows')
Inputs may be any that keep to these rules, and one draw needn't show every extreme that they name: `pattern`: slots 2 j and 2 j + 1 of block row i hold two different tile columns of panel (i // 8 + j - 2) mod (8), a panel being 8 consecutive block rows, for j = 0 to 4; slot 4 holds i itself.
All inputs are finite; a program needn't handle non-finite values.
Results may differ from a plain program's by a relative error of at most 0.012.
Values may be sent and summed in bfloat16 or wider, within the bound.
No kernel may reach another device: no remote copies, remote signals or barrier semaphores. Data moves between devices by JAX's collectives and lax.ppermute only.
A program may use at most 128 MiB of HBM per device.

v0:
```python
import functools

import jax
import jax.numpy as jnp
from jax import lax
from jax.experimental import pallas as pl
from jax.experimental.pallas import tpu as pltpu
from jax.sharding import PartitionSpec as P


HALF = 2
KP = 2
CLASSES = 2 * HALF

COST = 2**20
VMEM_LIMIT = 16 * 2**20


def down_offset(panel, kind):
    return (kind - panel + HALF) % CLASSES - HALF


def up_offset(panel, kind):
    return (kind - panel + HALF - 1) % CLASSES - HALF + 1


def classes_of(rep):
    return (rep % 2, rep % 2 + 2)


def route(panels, reps, target, kept=lambda panel, rep: True):
    pairs = []
    for rep in range(reps):
        for panel in range(panels):
            to_panel, to_rep = target(panel, rep)
            to_panel %= panels
            if kept(to_panel, to_rep):
                pairs.append((panel * reps + rep, to_panel * reps + to_rep))
    return pairs


def permute(block, pairs):
    return lax.ppermute(block, ("rows", "rep"), pairs)


def tile_table(pattern, device, blocks):
    count = pattern.shape[1]
    unit = blocks * KP
    even = device % 2 == 0
    mine = lax.dynamic_slice_in_dim(pattern, device * blocks, blocks, 0)
    rows = jnp.take(pattern, mine, axis=0, mode="clip")
    same = rows[:, :, :, None] == mine[:, None, None, :]
    slots = jnp.arange(count, dtype=jnp.int32)
    found = jnp.max(jnp.where(same, slots[None, None, :, None], -1), axis=2)
    offset = slots // KP - HALF
    turned = jnp.where(even, offset, -offset)
    far = jnp.where(turned == 1, 2, jnp.where(turned == -1, 3, jnp.where(turned == -HALF, 4, 5)))
    own = jnp.where((offset == HALF) == even, 0, 1)
    region = jnp.where(offset[:, None] == 0, own[None, :], far[:, None])
    place = region[None] * unit + (mine % blocks)[:, :, None] * KP + found % KP
    return jnp.where(found >= 0, place, 6 * unit).reshape(-1)


def product_kernel(first, aliased, facts, table, coeffs, left_hbm, *refs):
    sources, refs = refs[:6], refs[6 + aliased :]
    if first:
        full, main, extra, send0, send1, left, right, sums, baby, left_sems, in_sems, out_sem = refs
    else:
        full, main, extra, left, right, sums, left_sems, in_sems, out_sem = refs
    blocks, count, tile = left.shape[0], left.shape[1], left.shape[2]
    unit = blocks * KP
    loads = [
        pltpu.make_async_copy(source, right.at[pl.ds(k * unit, unit)], in_sems.at[k])
        for k, source in enumerate(sources)
    ]

    def left_load(i):
        return pltpu.make_async_copy(left_hbm.at[i], left.at[i], left_sems.at[i])

    for load in loads:
        load.start()
    for i in range(blocks):
        left_load(i).start()
    right[6 * unit] = jnp.zeros((tile, tile), right.dtype)
    offset = facts[0]
    even = facts[1]
    both = offset == -HALF
    for load in loads:
        load.wait()

    def out_copies(which, slot, i):
        copies = [(sums.at[which, i], full.at[i, pl.ds(slot, KP)])]
        if which == 0:
            copies.append((sums.at[0, i], main.at[i]))
        else:
            copies.append((sums.at[1, i], extra.at[i]))
        return [pltpu.make_async_copy(a, b, out_sem) for a, b in copies]

    def one_unit(which, slot, begin, end):
        def one_row(i, carry):
            if which == 0:
                left_load(i).wait()
            lefts = jnp.concatenate([left[i, s] for s in range(begin, end)], axis=1)
            rights = jnp.concatenate(
                [
                    jnp.concatenate(
                        [right[table[(i * count + s) * count + slot + e]] for e in range(KP)], axis=1
                    )
                    for s in range(begin, end)
                ],
                axis=0,
            )
            total = jnp.dot(lefts, rights, preferred_element_type=jnp.float32)
            rounded = total.astype(jnp.bfloat16)
            for e in range(KP):
                part = rounded[:, e * tile : (e + 1) * tile]
                sums[which, i, e] = part
                if first:
                    mixed = coeffs[1] * left[i, slot + e].astype(jnp.float32) + coeffs[
                        2
                    ] * part.astype(jnp.float32)
                    if e == 0:
                        on = jnp.where(slot == HALF * KP, coeffs[0], 0.0)
                        line = lax.broadcasted_iota(jnp.int32, (tile, tile), 0)
                        column = lax.broadcasted_iota(jnp.int32, (tile, tile), 1)
                        mixed = jnp.where(line == column, on, 0.0) + mixed
                    baby[which, i, e] = mixed.astype(jnp.bfloat16)
            for copy in out_copies(which, slot, i):
                copy.start()
            return carry

        lax.fori_loop(0, blocks, one_row, 0)

    low = pl.multiple_of((offset + HALF) * KP, KP)
    high = 2 * HALF * KP
    for o in range(-HALF, HALF):

        @pl.when(offset == o)
        def _(o=o):
            begin = max(0, o) * KP
            end = (2 * HALF + 1 + min(0, o)) * KP
            one_unit(0, (o + HALF) * KP, begin, end)
            if o == -HALF:
                one_unit(1, high, HALF * KP, count)

    tail = []
    if first:
        upper = jnp.where(both, 1, 0)
        tail = [
            pltpu.make_async_copy(baby.at[jnp.where(even == 1, upper, 0)], send0, in_sems.at[0]),
            pltpu.make_async_copy(baby.at[jnp.where(even == 1, 0, upper)], send1, in_sems.at[1]),
        ]
    for copy in tail:
        copy.start()
    for copy in tail:
        copy.wait()
    for i in range(blocks):
        for copy in out_copies(0, low, i):
            copy.wait()

    @pl.when(both)
    def _():
        for i in range(blocks):
            for copy in out_copies(1, high, i):
                copy.wait()


def product(first, facts, table, coeffs, left, rights, full):
    blocks, tile = left.shape[0], left.shape[2]
    unit = blocks * KP
    unit_shape = jax.ShapeDtypeStruct((blocks, KP, tile, tile), left.dtype)
    whole = jax.ShapeDtypeStruct(left.shape, left.dtype)
    smem = pl.BlockSpec(memory_space=pltpu.SMEM)
    hbm = pl.BlockSpec(memory_space=pl.ANY)
    flat = [r.reshape(unit, tile, tile) for r in rights]
    outs = [whole] + [unit_shape] * (4 if first else 2)
    pair = pltpu.VMEM((2, blocks, KP, tile, tile), left.dtype)
    operands = [facts, table, coeffs, left] + flat
    if full is not None:
        operands.append(full)
    return pl.pallas_call(
        functools.partial(product_kernel, first, full is not None),
        out_shape=outs,
        in_specs=[smem] * 3 + [hbm] * (len(operands) - 3),
        out_specs=[pl.BlockSpec(memory_space=pltpu.HBM)] * len(outs),
        scratch_shapes=[
            pltpu.VMEM(left.shape, left.dtype),
            pltpu.VMEM((6 * unit + 1, tile, tile), left.dtype),
            pair,
        ]
        + ([pair] if first else [])
        + [
            pltpu.SemaphoreType.DMA((blocks,)),
            pltpu.SemaphoreType.DMA((6,)),
            pltpu.SemaphoreType.DMA,
        ],
        input_output_aliases={} if full is None else {len(operands) - 1: 0},
        compiler_params=pltpu.CompilerParams(vmem_limit_bytes=VMEM_LIMIT),
        name="product_first" if first else "product_second",
        cost_estimate=pl.CostEstimate(flops=COST, bytes_accessed=2**23, transcendentals=0),
    )(*operands)


def place_kernel(facts, full_in, main, extra, full, held, sems):
    del full_in
    offset = facts[0]
    low = pl.multiple_of((offset + HALF) * KP, KP)
    high = 2 * HALF * KP
    blocks = held.shape[1]
    half = blocks // 2
    both = offset == -HALF

    def rows(k):
        return pl.ds(k * half, half)

    def load(which, k):
        source = main if which == 0 else extra
        return pltpu.make_async_copy(source.at[rows(k)], held.at[which, rows(k)], sems.at[which, k])

    def store(which, k):
        slot = low if which == 0 else high
        return pltpu.make_async_copy(
            held.at[which, rows(k)], full.at[rows(k), pl.ds(slot, KP)], sems.at[which, k]
        )

    def run(units):
        steps = [(which, k) for which in units for k in range(2)]
        for step in steps:
            load(*step).start()
        for step in steps:
            load(*step).wait()
            store(*step).start()
        for step in steps:
            store(*step).wait()

    @pl.when(both)
    def _():
        run((0, 1))

    @pl.when(jnp.logical_not(both))
    def _():
        run((0,))


def place(facts, full, main, extra):
    hbm = pl.BlockSpec(memory_space=pl.ANY)
    return pl.pallas_call(
        place_kernel,
        out_shape=jax.ShapeDtypeStruct(full.shape, full.dtype),
        in_specs=[pl.BlockSpec(memory_space=pltpu.SMEM), hbm, hbm, hbm],
        out_specs=hbm,
        scratch_shapes=[
            pltpu.VMEM((2,) + main.shape, main.dtype),
            pltpu.SemaphoreType.DMA((2, 2)),
        ],
        input_output_aliases={1: 0},
        compiler_params=pltpu.CompilerParams(vmem_limit_bytes=VMEM_LIMIT),
        name="place",
        cost_estimate=pl.CostEstimate(flops=COST, bytes_accessed=2**21, transcendentals=0),
    )(facts, full, main, extra)


def local(x_tiles, giant_tiles, coeffs, pattern):
    blocks = x_tiles.shape[0]
    panels = lax.axis_size("rows")
    reps = lax.axis_size("rep")
    device = lax.axis_index("rows")
    rep = lax.axis_index("rep")
    even = device % 2 == 0

    def swapped(panel):
        return panel + 1 if panel % 2 == 0 else panel - 1

    core_route = route(panels, reps, lambda p, z: (swapped(p), z))
    near_route = route(panels, reps, lambda p, z: (p - 1 if p % 2 == 0 else p + 1, z))

    def two_route(chunk):
        return route(
            panels,
            reps,
            lambda p, z: (p + 2 if p % 2 == 0 else p - 2, z),
            lambda p, z: (classes_of(z)[chunk] - p) % CLASSES != (1 if p % 2 == 0 else 3),
        )

    partner_route = route(panels, reps, lambda p, z: (p, z ^ 1))

    def extra_route(chunk):
        return route(
            panels,
            reps,
            lambda p, z: (p, z ^ 1),
            lambda p, z: down_offset(p, classes_of(z ^ 1)[chunk]) == -HALF,
        )

    def gathered(chunk, send0, send1):
        near = permute(send1, near_route)
        two = permute(send0, two_route(chunk))
        core = permute(send0, core_route)
        forwarded = permute(near, core_route)
        return (send0, send1, core, near, two, forwarded)

    def swapped_parts(chunk, main, extra):
        main = permute(main, partner_route)
        extra = permute(extra, extra_route(chunk))
        return main, extra

    def facts_of(kind):
        return jnp.stack([down_offset(device, kind), even.astype(jnp.int32)]).astype(jnp.int32)

    kinds = classes_of(rep)
    others = classes_of(1 - rep % 2)
    rights = []
    for chunk in range(2):
        up = (up_offset(device, kinds[chunk]) + HALF) * KP
        down = (down_offset(device, kinds[chunk]) + HALF) * KP
        send0 = lax.dynamic_slice_in_dim(x_tiles, jnp.where(even, up, down), KP, 1)
        send1 = lax.dynamic_slice_in_dim(x_tiles, jnp.where(even, down, up), KP, 1)
        rights.append(gathered(chunk, send0, send1))
    table = tile_table(pattern, device, blocks)

    squared = None
    result = None
    babies = []
    arrived = []
    for chunk in range(2):
        squared, main, extra, send0, send1 = product(
            True, facts_of(kinds[chunk]), table, coeffs, x_tiles, rights[chunk], squared
        )
        babies.append(gathered(chunk, send0, send1))
        arrived.append(swapped_parts(chunk, main, extra))
    for chunk in range(2):
        squared = place(facts_of(others[chunk]), squared, *arrived[chunk])
    arrived = []
    for chunk in range(2):
        result, main, extra = product(
            False, facts_of(kinds[chunk]), table, coeffs, giant_tiles, babies[chunk], result
        )
        arrived.append(swapped_parts(chunk, main, extra))
    for chunk in range(2):
        result = place(facts_of(others[chunk]), result, *arrived[chunk])
    return (squared, result)


def solution(mesh):
    return jax.shard_map(
        local,
        mesh=mesh,
        in_specs=(P("rows", None, None, None), P("rows", None, None, None), P(), P()),
        out_specs=(P("rows", None, None, None), P("rows", None, None, None)),
        check_vma=False,
    )
```

profile of v0, /device:TPU:1, one launch (start us, length us, event | category | flops | bytes accessed | tf_op | source)
XLA Modules:
  0.0 156.9 jit_solution(12412921861935254249)
XLA Ops:
  0.8 2.9 %constant_dynamic-slice_fusion = (bf16[8,2,128,128]{3,2,1,0:T(8,128)(2,1)}, bf16[8,2,128,128]{3,2,1,0:T(8,128)(2,1)}, bf16[8,2,128,128]{3,2,1,0:T(8,128)(2,1)S(1)}, bf16[8,2,128,128]{3,2,1,0:T(8,128)(2,1)}) fusion(bf16[8,10,128,128]{3,2,1,0:T(8,128)(2,1)} %left_hbm.5, s32[]{:T(128)S(6)} %select_n.206, s32[]{:T(128)S(6)} %select_n.204, s32[]{:T(128)S(6)} %select_n.200, ...), kind=kLoop, calls=%fused_computation.21 | loop fusion | bytes 4194320 | tf_op jit(solution)/shard_map/dynamic_slice | solution.py:317
  3.6 5.7 %collective-permute-start.6 = (bf16[8,2,128,128]{3,2,1,0:T(8,128)(2,1)}, bf16[8,2,128,128]{3,2,1,0:T(8,128)(2,1)}, u32[]{:S(2)}, u32[]{:S(2)}) collective-permute-start(bf16[8,2,128,128]{3,2,1,0:T(8,128)(2,1)} %get-tuple-element.37), channel_id=1, source_target_pairs={{0,8},{4,28},{8,16},{16,24},{20,12},{24,0},{1,9},{5,29},{13,5},{17... | collective-permute-start | bytes 1572872 | tf_op jit(solution)/shard_map/ppermute | solution.py:43
  9.8 1.3 collective-permute-start.1
  11.1 1.3 collective-permute-start.2
  14.0 18.7 %collective-permute-done.5 = bf16[8,2,128,128]{3,2,1,0:T(8,128)(2,1)} collective-permute-done((bf16[8,2,128,128]{3,2,1,0:T(8,128)(2,1)}, bf16[8,2,128,128]{3,2,1,0:T(8,128)(2,1)}, u32[]{:S(2)}, u32[]{:S(2)}) %collective-permute-start.5) | collective-permute-done | bytes 524320 | tf_op jit(solution)/shard_map/ppermute | solution.py:43
  32.9 11.0 %collective-permute-done.1 = bf16[8,2,128,128]{3,2,1,0:T(8,128)(2,1)} collective-permute-done((bf16[8,2,128,128]{3,2,1,0:T(8,128)(2,1)S(1)}, bf16[8,2,128,128]{3,2,1,0:T(8,128)(2,1)}, u32[]{:S(2)}, u32[]{:S(2)}) %collective-permute-start.1) | collective-permute-done | bytes 524320 | tf_op jit(solution)/shard_map/ppermute | solution.py:43
  44.5 6.1 %product_first.2 = (bf16[8,10,128,128]{3,2,1,0:T(8,128)(2,1)}, bf16[8,2,128,128]{3,2,1,0:T(8,128)(2,1)S(1)}, bf16[8,2,128,128]{3,2,1,0:T(8,128)(2,1)S(1)}, bf16[...) custom-call(s32[2]{0:T(128)S(1)} %pad_add_fusion.3.facts, s32[800]{0:T(1024)S(1)} %fusion.4.table, f32[3]{0:T(128)S(1)} %copy-done.4, ...), custom_call_target="tpu_custom_call" | custom-call | flops 1048576 | bytes 8388608 | tf_op jit(solution)/shard_map/product_first/pallas_call | solution.py:181
  50.6 0.8 copy-done.2
  53.0 3.9 %collective-permute-start.17 = (bf16[8,2,128,128]{3,2,1,0:T(8,128)(2,1)}, bf16[8,2,128,128]{3,2,1,0:T(8,128)(2,1)}, u32[]{:S(2)}, u32[]{:S(2)}) collective-permute-start(bf16[8,2,128,128]{3,2,1,0:T(8,128)(2,1)} %get-tuple-element.27), channel_id=1, source_target_pairs={{0,28},{4,8},{8,4},{12,16},{16,12},{20,24},{24,20},{28,0},{1,29},{... | collective-permute-start | bytes 1572872 | tf_op jit(solution)/shard_map/ppermute | solution.py:43
  57.0 5.9 %product_first.3 = (bf16[8,10,128,128]{3,2,1,0:T(8,128)(2,1)}, bf16[8,2,128,128]{3,2,1,0:T(8,128)(2,1)S(1)}, bf16[8,2,128,128]{3,2,1,0:T(8,128)(2,1)}, bf16[8,2,...) custom-call(s32[2]{0:T(128)S(1)} %pad_add_fusion.2.facts, ...), custom_call_target="tpu_custom_call", output_to_operand_aliasing={{0}: (10, {})} | custom-call | flops 1048576 | bytes 8388608 | tf_op jit(solution)/shard_map/product_first/pallas_call | solution.py:181
  63.3 1.3 collective-permute-start.14
  64.6 4.4 %collective-permute-start.18 = (bf16[8,2,128,128]{3,2,1,0:T(8,128)(2,1)S(1)}, bf16[8,2,128,128]{3,2,1,0:T(8,128)(2,1)S(1)}, u32[]{:S(2)}, u32[]{:S(2)}) collective-permute-start(bf16[8,2,128,128]{3,2,1,0:T(8,128)(2,1)S(1)} %copy-done.3), channel_id=1, source_target_pairs={{0,8},{4,28},{8,16},{16,24},{20,12},{24,0},{1,9},{5,29},{13,5},{17... | collective-permute-start | bytes 1572872 | tf_op jit(solution)/shard_map/ppermute | solution.py:43
  69.6 10.5 %collective-permute-done.13 = bf16[8,2,128,128]{3,2,1,0:T(8,128)(2,1)S(1)} collective-permute-done((bf16[8,2,128,128]{3,2,1,0:T(8,128)(2,1)S(1)}, bf16[8,2,128,128]{3,2,1,0:T(8,128)(2,1)S(1)}, u32[]{:S(2)}, u32[]{:S(2)}) %collective-permute-start.13) | collective-permute-done | bytes 524320 | tf_op jit(solution)/shard_map/ppermute | solution.py:43
  80.1 8.3 %collective-permute-done.14 = bf16[8,2,128,128]{3,2,1,0:T(8,128)(2,1)S(1)} collective-permute-done((bf16[8,2,128,128]{3,2,1,0:T(8,128)(2,1)S(1)}, bf16[8,2,128,128]{3,2,1,0:T(8,128)(2,1)S(1)}, u32[]{:S(2)}, u32[]{:S(2)}) %collective-permute-start.14) | collective-permute-done | bytes 524320 | tf_op jit(solution)/shard_map/ppermute | solution.py:43
  88.4 2.7 %collective-permute-start.15 = (bf16[8,2,128,128]{3,2,1,0:T(8,128)(2,1)S(1)}, bf16[8,2,128,128]{3,2,1,0:T(8,128)(2,1)S(1)}, u32[]{:S(2)}, u32[]{:S(2)}) collective-permute-start(bf16[8,2,128,128]{3,2,1,0:T(8,128)(2,1)S(1)} %collective-permute-done.13), channel_id=1, source_target_pairs={{0,4},{4,0},{8,12},{12,8},{16,20},{20,16},{24,28},{28,24},{1,5},{5... | collective-permute-start | bytes 1572872 | tf_op jit(solution)/shard_map/ppermute | solution.py:43
  91.3 5.8 %collective-permute-start.10 = (bf16[8,2,128,128]{3,2,1,0:T(8,128)(2,1)S(1)}, bf16[8,2,128,128]{3,2,1,0:T(8,128)(2,1)S(1)}, u32[]{:S(2)}, u32[]{:S(2)}) collective-permute-start(bf16[8,2,128,128]{3,2,1,0:T(8,128)(2,1)S(1)} %get-tuple-element.22), channel_id=1, source_target_pairs={{0,1},{4,5},{8,9},{12,13},{16,17},{20,21},{24,25},{28,29},{1,0},{5... | collective-permute-start | bytes 1572872 | tf_op jit(solution)/shard_map/ppermute | solution.py:43
  97.9 4.5 %product_second.2 = (bf16[8,10,128,128]{3,2,1,0:T(8,128)(2,1)}, bf16[8,2,128,128]{3,2,1,0:T(8,128)(2,1)}, bf16[8,2,128,128]{3,2,1,0:T(8,128)(2,1)}) custom-call(s32[2]{0:T(128)S(1)} %pad_add_fusion.3.facts, s32[800]{0:T(1024)S(1)} %fusion.4.table, f32[3]{0:T(128)S(1)} %copy-done.4, bf16[8,10,128,128]{3,2,1,0:T(8,128)(2,1)S(1)} %copy-done.1, ...), custom_call_target="tpu_custom_call" | custom-call | flops 1048576 | bytes 8388608 | tf_op jit(solution)/shard_map/product_second/pallas_call | solution.py:181
  102.5 1.3 collective-permute-start.11
  103.8 2.2 %collective-permute-start.20 = (bf16[8,2,128,128]{3,2,1,0:T(8,128)(2,1)}, bf16[8,2,128,128]{3,2,1,0:T(8,128)(2,1)S(1)}, u32[]{:S(2)}, u32[]{:S(2)}) collective-permute-start(bf16[8,2,128,128]{3,2,1,0:T(8,128)(2,1)} %get-tuple-element.30), channel_id=1, source_target_pairs={{0,1},{4,5},{8,9},{12,13},{16,17},{20,21},{24,25},{28,29},{1,0},{5... | collective-permute-start | bytes 1572872 | tf_op jit(solution)/shard_map/ppermute | solution.py:43
  106.0 4.4 %product_second.3 = (bf16[8,10,128,128]{3,2,1,0:T(8,128)(2,1)}, bf16[8,2,128,128]{3,2,1,0:T(8,128)(2,1)}, bf16[8,2,128,128]{3,2,1,0:T(8,128)(2,1)}) custom-call(s32[2]{0:T(128)S(1)} %pad_add_fusion.2.facts, s32[800]{0:T(1024)S(1)} %fusion.4.table, f32[3]{0:T(128)S(1)} %copy-done.4, ...), custom_call_target="tpu_custom_call", output_to_operand_aliasing={{0}: (10, {})} | custom-call | flops 1048576 | bytes 8388608 | tf_op jit(solution)/shard_map/product_second/pallas_call | solution.py:181
  110.4 1.5 collective-permute-start.21
  111.8 8.3 %collective-permute-done.8.main = bf16[8,2,128,128]{3,2,1,0:T(8,128)(2,1)S(1)} collective-permute-done((bf16[8,2,128,128]{3,2,1,0:T(8,128)(2,1)S(1)}, bf16[8,2,128,128]{3,2,1,0:T(8,128)(2,1)S(1)}, u32[]{:S(2)}, u32[]{:S(2)}) %collective-permute-start.8) | collective-permute-done | bytes 524320 | tf_op jit(solution)/shard_map/ppermute | solution.py:43
  120.1 2.2 %collective-permute-start.22 = (bf16[8,2,128,128]{3,2,1,0:T(8,128)(2,1)}, bf16[8,2,128,128]{3,2,1,0:T(8,128)(2,1)S(1)}, u32[]{:S(2)}, u32[]{:S(2)}) collective-permute-start(bf16[8,2,128,128]{3,2,1,0:T(8,128)(2,1)} %get-tuple-element.32), channel_id=1, source_target_pairs={{0,1},{4,5},{8,9},{12,13},{16,17},{20,21},{24,25},{28,29},{1,0},{5... | collective-permute-start | bytes 1572872 | tf_op jit(solution)/shard_map/ppermute | solution.py:43
  122.3 1.3 collective-permute-start.23
  123.7 1.4 place.4.full_in
  125.2 5.4 %collective-permute-done.11.extra = bf16[8,2,128,128]{3,2,1,0:T(8,128)(2,1)S(1)} collective-permute-done((bf16[8,2,128,128]{3,2,1,0:T(8,128)(2,1)}, bf16[8,2,128,128]{3,2,1,0:T(8,128)(2,1)S(1)}, u32[]{:S(2)}, u32[]{:S(2)}) %collective-permute-start.11) | collective-permute-done | bytes 524320 | tf_op jit(solution)/shard_map/ppermute | solution.py:43
  130.6 1.6 %place.5 = bf16[8,10,128,128]{3,2,1,0:T(8,128)(2,1)} custom-call(s32[2]{0:T(128)S(1)} %get-tuple-element.42.facts, bf16[8,10,128,128]{3,2,1,0:T(8,128)(2,1)} %place.4.full_in, bf16[8,2,128,128]{3,2,1,0:T(8,128)(2,1)S(1)} %collective-permute-done.10.main, bf16[8,2,128,128]{3,2,1,0:T(8,128)(2,1)S(1)} %collective-permute-done.11.extra), custom_call_target="tpu_custom_call", output_to_operand_aliasing={{}: (1, {})} | custom-call | flops 1048576 | bytes 2097152 | tf_op jit(solution)/shard_map/place/pallas_call | solution.py:247
  132.2 9.6 %collective-permute-done.20.main = bf16[8,2,128,128]{3,2,1,0:T(8,128)(2,1)S(1)} collective-permute-done((bf16[8,2,128,128]{3,2,1,0:T(8,128)(2,1)}, bf16[8,2,128,128]{3,2,1,0:T(8,128)(2,1)S(1)}, u32[]{:S(2)}, u32[]{:S(2)}) %collective-permute-start.20) | collective-permute-done | bytes 524320 | tf_op jit(solution)/shard_map/ppermute | solution.py:43
  141.8 1.4 place.6.full_in
  143.3 5.4 %collective-permute-done.22.main = bf16[8,2,128,128]{3,2,1,0:T(8,128)(2,1)S(1)} collective-permute-done((bf16[8,2,128,128]{3,2,1,0:T(8,128)(2,1)}, bf16[8,2,128,128]{3,2,1,0:T(8,128)(2,1)S(1)}, u32[]{:S(2)}, u32[]{:S(2)}) %collective-permute-start.22) | collective-permute-done | bytes 524320 | tf_op jit(solution)/shard_map/ppermute | solution.py:43
  148.7 5.7 %collective-permute-done.23.extra = bf16[8,2,128,128]{3,2,1,0:T(8,128)(2,1)} collective-permute-done((bf16[8,2,128,128]{3,2,1,0:T(8,128)(2,1)}, bf16[8,2,128,128]{3,2,1,0:T(8,128)(2,1)}, u32[]{:S(2)}, u32[]{:S(2)}) %collective-permute-start.23) | collective-permute-done | bytes 524320 | tf_op jit(solution)/shard_map/ppermute | solution.py:43
  154.4 2.5 %place.7 = bf16[8,10,128,128]{3,2,1,0:T(8,128)(2,1)} custom-call(s32[2]{0:T(128)S(1)} %get-tuple-element.42.facts, bf16[8,10,128,128]{3,2,1,0:T(8,128)(2,1)} %place.6.full_in, bf16[8,2,128,128]{3,2,1,0:T(8,128)(2,1)S(1)} %collective-permute-done.22.main, bf16[8,2,128,128]{3,2,1,0:T(8,128)(2,1)} %collective-permute-done.23.extra), custom_call_target="tpu_custom_call", output_to_operand_aliasing={{}: (1, {})} | custom-call | flops 1048576 | bytes 2097152 | tf_op jit(solution)/shard_map/place/pallas_call | solution.py:247
  (65 shorter events, 6.5 us)
Async XLA Ops:
  0.6 11.8 %copy-start.9 = (s32[64,10]{0,1:T(8,128)S(1)}, s32[64,10]{0,1:T(8,128)}, u32[]{:S(2)}) copy-start(s32[64,10]{0,1:T(8,128)} %param.7) | copy-start | bytes 7684
  0.8 43.8 %copy-start = (bf16[8,10,128,128]{3,2,1,0:T(8,128)(2,1)S(1)}, bf16[8,10,128,128]{3,2,1,0:T(8,128)(2,1)}, u32[]{:S(2)}) copy-start(bf16[8,10,128,128]{3,2,1,0:T(8,128)(2,1)} %left_hbm.5) | copy-start | bytes 7864324
  0.8 43.8 %copy-start.4 = (f32[3]{0:T(128)S(1)}, f32[3]{0:T(128)}, u32[]{:S(2)}) copy-start(f32[3]{0:T(128)} %coeffs.7) | copy-start | bytes 40
  3.6 40.3 %collective-permute-start.6 = (bf16[8,2,128,128]{3,2,1,0:T(8,128)(2,1)}, bf16[8,2,128,128]{3,2,1,0:T(8,128)(2,1)}, u32[]{:S(2)}, u32[]{:S(2)}) collective-permute-start(bf16[8,2,128,128]{3,2,1,0:T(8,128)(2,1)} %get-tuple-element.37), channel_id=1, source_target_pairs={{0,8},{4,28},{8,16},{16,24},{20,12},{24,0},{1,9},{5,29},{13,5},{17... | collective-permute-start | bytes 1572872 | tf_op jit(solution)/shard_map/ppermute | solution.py:43
  9.3 35.2 %collective-permute-start.4 = (bf16[8,2,128,128]{3,2,1,0:T(8,128)(2,1)}, bf16[8,2,128,128]{3,2,1,0:T(8,128)(2,1)}, u32[]{:S(2)}, u32[]{:S(2)}) collective-permute-start(bf16[8,2,128,128]{3,2,1,0:T(8,128)(2,1)} %get-tuple-element.37), channel_id=1, source_target_pairs={{0,4},{4,0},{8,12},{12,8},{16,20},{20,16},{24,28},{28,24},{1,5},{5... | collective-permute-start | bytes 1572872 | tf_op jit(solution)/shard_map/ppermute | solution.py:43
  9.3 23.3 %collective-permute-start.5 = (bf16[8,2,128,128]{3,2,1,0:T(8,128)(2,1)}, bf16[8,2,128,128]{3,2,1,0:T(8,128)(2,1)}, u32[]{:S(2)}, u32[]{:S(2)}) collective-permute-start(bf16[8,2,128,128]{3,2,1,0:T(8,128)(2,1)} %get-tuple-element.36), channel_id=1, source_target_pairs={{0,28},{4,8},{8,4},{12,16},{16,12},{20,24},{24,20},{28,0},{1,29},{... | collective-permute-start | bytes 1572872 | tf_op jit(solution)/shard_map/ppermute | solution.py:43
  9.8 34.1 %collective-permute-start.1 = (bf16[8,2,128,128]{3,2,1,0:T(8,128)(2,1)S(1)}, bf16[8,2,128,128]{3,2,1,0:T(8,128)(2,1)}, u32[]{:S(2)}, u32[]{:S(2)}) collective-permute-start(bf16[8,2,128,128]{3,2,1,0:T(8,128)(2,1)S(1)} %get-tuple-element.38), channel_id=1, source_target_pairs={{0,28},{4,8},{8,4},{12,16},{16,12},{20,24},{24,20},{28,0},{1,29},{... | collective-permute-start | bytes 1572872 | tf_op jit(solution)/shard_map/ppermute | solution.py:43
  11.1 45.9 %collective-permute-start.2 = (bf16[8,2,128,128]{3,2,1,0:T(8,128)(2,1)}, bf16[8,2,128,128]{3,2,1,0:T(8,128)(2,1)}, u32[]{:S(2)}, u32[]{:S(2)}) collective-permute-start(bf16[8,2,128,128]{3,2,1,0:T(8,128)(2,1)} %get-tuple-element.39), channel_id=1, source_target_pairs={{0,8},{8,16},{12,4},{16,24},{24,0},{28,20},{5,29},{9,17},{13,5},{2... | collective-permute-start | bytes 1572872 | tf_op jit(solution)/shard_map/ppermute | solution.py:43
  32.7 11.8 %collective-permute-start.7 = (bf16[8,2,128,128]{3,2,1,0:T(8,128)(2,1)}, bf16[8,2,128,128]{3,2,1,0:T(8,128)(2,1)}, u32[]{:S(2)}, u32[]{:S(2)}) collective-permute-start(bf16[8,2,128,128]{3,2,1,0:T(8,128)(2,1)} %collective-permute-done.5), channel_id=1, source_target_pairs={{0,4},{4,0},{8,12},{12,8},{16,20},{20,16},{24,28},{28,24},{1,5},{5... | collective-permute-start | bytes 1572872 | tf_op jit(solution)/shard_map/ppermute | solution.py:43
  43.9 13.1 %collective-permute-start = (bf16[8,2,128,128]{3,2,1,0:T(8,128)(2,1)}, bf16[8,2,128,128]{3,2,1,0:T(8,128)(2,1)}, u32[]{:S(2)}, u32[]{:S(2)}) collective-permute-start(bf16[8,2,128,128]{3,2,1,0:T(8,128)(2,1)} %get-tuple-element.39), channel_id=1, source_target_pairs={{0,4},{4,0},{8,12},{12,8},{16,20},{20,16},{24,28},{28,24},{1,5},{5... | collective-permute-start | bytes 1572872 | tf_op jit(solution)/shard_map/ppermute | solution.py:43
  43.9 13.1 %collective-permute-start.3 = (bf16[8,2,128,128]{3,2,1,0:T(8,128)(2,1)}, bf16[8,2,128,128]{3,2,1,0:T(8,128)(2,1)}, u32[]{:S(2)}, u32[]{:S(2)}) collective-permute-start(bf16[8,2,128,128]{3,2,1,0:T(8,128)(2,1)} %collective-permute-done.1), channel_id=1, source_target_pairs={{0,4},{4,0},{8,12},{12,8},{16,20},{20,16},{24,28},{28,24},{1,5},{5... | collective-permute-start | bytes 1572872 | tf_op jit(solution)/shard_map/ppermute | solution.py:43
  50.6 0.8 copy-start.2
  53.0 16.2 %collective-permute-start.17 = (bf16[8,2,128,128]{3,2,1,0:T(8,128)(2,1)}, bf16[8,2,128,128]{3,2,1,0:T(8,128)(2,1)}, u32[]{:S(2)}, u32[]{:S(2)}) collective-permute-start(bf16[8,2,128,128]{3,2,1,0:T(8,128)(2,1)} %get-tuple-element.27), channel_id=1, source_target_pairs={{0,28},{4,8},{8,4},{12,16},{16,12},{20,24},{24,20},{28,0},{1,29},{... | collective-permute-start | bytes 1572872 | tf_op jit(solution)/shard_map/ppermute | solution.py:43
  57.0 7.6 %copy-start.3 = (bf16[8,2,128,128]{3,2,1,0:T(8,128)(2,1)S(1)}, bf16[8,2,128,128]{3,2,1,0:T(8,128)(2,1)}, u32[]{:S(2)}) copy-start(bf16[8,2,128,128]{3,2,1,0:T(8,128)(2,1)} %copy-done.2) | copy-start | bytes 1572868
  57.0 40.2 %copy-start.8 = (bf16[8,2,128,128]{3,2,1,0:T(8,128)(2,1)S(1)}, bf16[8,2,128,128]{3,2,1,0:T(8,128)(2,1)}, u32[]{:S(2)}) copy-start(bf16[8,2,128,128]{3,2,1,0:T(8,128)(2,1)} %copy-done.7) | copy-start | bytes 1572868
  57.0 40.2 %copy-start.6 = (bf16[8,2,128,128]{3,2,1,0:T(8,128)(2,1)S(1)}, bf16[8,2,128,128]{3,2,1,0:T(8,128)(2,1)}, u32[]{:S(2)}) copy-start(bf16[8,2,128,128]{3,2,1,0:T(8,128)(2,1)} %copy-done.5) | copy-start | bytes 1572868
  57.0 40.9 %copy-start.1 = (bf16[8,10,128,128]{3,2,1,0:T(8,128)(2,1)S(1)}, bf16[8,10,128,128]{3,2,1,0:T(8,128)(2,1)}, u32[]{:S(2)}) copy-start(bf16[8,10,128,128]{3,2,1,0:T(8,128)(2,1)} %left_hbm.7) | copy-start | bytes 7864324
  63.0 17.1 %collective-permute-start.13 = (bf16[8,2,128,128]{3,2,1,0:T(8,128)(2,1)S(1)}, bf16[8,2,128,128]{3,2,1,0:T(8,128)(2,1)S(1)}, u32[]{:S(2)}, u32[]{:S(2)}) collective-permute-start(bf16[8,2,128,128]{3,2,1,0:T(8,128)(2,1)S(1)} %get-tuple-element.25), channel_id=1, source_target_pairs={{0,28},{4,8},{8,4},{12,16},{16,12},{20,24},{24,20},{28,0},{1,29},{... | collective-permute-start | bytes 1572872 | tf_op jit(solution)/shard_map/ppermute | solution.py:43
  63.3 25.1 %collective-permute-start.14 = (bf16[8,2,128,128]{3,2,1,0:T(8,128)(2,1)S(1)}, bf16[8,2,128,128]{3,2,1,0:T(8,128)(2,1)S(1)}, u32[]{:S(2)}, u32[]{:S(2)}) collective-permute-start(bf16[8,2,128,128]{3,2,1,0:T(8,128)(2,1)S(1)} %get-tuple-element.24), channel_id=1, source_target_pairs={{0,8},{8,16},{12,4},{16,24},{24,0},{28,20},{5,29},{9,17},{13,5},{2... | collective-permute-start | bytes 1572872 | tf_op jit(solution)/shard_map/ppermute | solution.py:43
  64.6 26.7 %collective-permute-start.18 = (bf16[8,2,128,128]{3,2,1,0:T(8,128)(2,1)S(1)}, bf16[8,2,128,128]{3,2,1,0:T(8,128)(2,1)S(1)}, u32[]{:S(2)}, u32[]{:S(2)}) collective-permute-start(bf16[8,2,128,128]{3,2,1,0:T(8,128)(2,1)S(1)} %copy-done.3), channel_id=1, source_target_pairs={{0,8},{4,28},{8,16},{16,24},{20,12},{24,0},{1,9},{5,29},{13,5},{17... | collective-permute-start | bytes 1572872 | tf_op jit(solution)/shard_map/ppermute | solution.py:43
  69.0 28.1 %collective-permute-start.16 = (bf16[8,2,128,128]{3,2,1,0:T(8,128)(2,1)S(1)}, bf16[8,2,128,128]{3,2,1,0:T(8,128)(2,1)S(1)}, u32[]{:S(2)}, u32[]{:S(2)}) collective-permute-start(bf16[8,2,128,128]{3,2,1,0:T(8,128)(2,1)S(1)} %copy-done.3), channel_id=1, source_target_pairs={{0,4},{4,0},{8,12},{12,8},{16,20},{20,16},{24,28},{28,24},{1,5},{5... | collective-permute-start | bytes 1572872 | tf_op jit(solution)/shard_map/ppermute | solution.py:43
  69.3 28.0 %collective-permute-start.19 = (bf16[8,2,128,128]{3,2,1,0:T(8,128)(2,1)}, bf16[8,2,128,128]{3,2,1,0:T(8,128)(2,1)S(1)}, u32[]{:S(2)}, u32[]{:S(2)}) collective-permute-start(bf16[8,2,128,128]{3,2,1,0:T(8,128)(2,1)} %collective-permute-done.17), channel_id=1, source_target_pairs={{0,4},{4,0},{8,12},{12,8},{16,20},{20,16},{24,28},{28,24},{1,5},{5... | collective-permute-start | bytes 1572872 | tf_op jit(solution)/shard_map/ppermute | solution.py:43
  80.1 22.4 %collective-permute-start.12 = (bf16[8,2,128,128]{3,2,1,0:T(8,128)(2,1)S(1)}, bf16[8,2,128,128]{3,2,1,0:T(8,128)(2,1)S(1)}, u32[]{:S(2)}, u32[]{:S(2)}) collective-permute-start(bf16[8,2,128,128]{3,2,1,0:T(8,128)(2,1)S(1)} %get-tuple-element.24), channel_id=1, source_target_pairs={{0,4},{4,0},{8,12},{12,8},{16,20},{20,16},{24,28},{28,24},{1,5},{5... | collective-permute-start | bytes 1572872 | tf_op jit(solution)/shard_map/ppermute | solution.py:43
  88.4 15.4 %collective-permute-start.15 = (bf16[8,2,128,128]{3,2,1,0:T(8,128)(2,1)S(1)}, bf16[8,2,128,128]{3,2,1,0:T(8,128)(2,1)S(1)}, u32[]{:S(2)}, u32[]{:S(2)}) collective-permute-start(bf16[8,2,128,128]{3,2,1,0:T(8,128)(2,1)S(1)} %collective-permute-done.13), channel_id=1, source_target_pairs={{0,4},{4,0},{8,12},{12,8},{16,20},{20,16},{24,28},{28,24},{1,5},{5... | collective-permute-start | bytes 1572872 | tf_op jit(solution)/shard_map/ppermute | solution.py:43
  91.3 19.0 %collective-permute-start.10 = (bf16[8,2,128,128]{3,2,1,0:T(8,128)(2,1)S(1)}, bf16[8,2,128,128]{3,2,1,0:T(8,128)(2,1)S(1)}, u32[]{:S(2)}, u32[]{:S(2)}) collective-permute-start(bf16[8,2,128,128]{3,2,1,0:T(8,128)(2,1)S(1)} %get-tuple-element.22), channel_id=1, source_target_pairs={{0,1},{4,5},{8,9},{12,13},{16,17},{20,21},{24,25},{28,29},{1,0},{5... | collective-permute-start | bytes 1572872 | tf_op jit(solution)/shard_map/ppermute | solution.py:43
  97.2 23.0 %collective-permute-start.8 = (bf16[8,2,128,128]{3,2,1,0:T(8,128)(2,1)S(1)}, bf16[8,2,128,128]{3,2,1,0:T(8,128)(2,1)S(1)}, u32[]{:S(2)}, u32[]{:S(2)}) collective-permute-start(bf16[8,2,128,128]{3,2,1,0:T(8,128)(2,1)S(1)} %copy-done.8), channel_id=1, source_target_pairs={{0,1},{4,5},{8,9},{12,13},{16,17},{20,21},{24,25},{28,29},{1,0},{5... | collective-permute-start | bytes 1572872 | tf_op jit(solution)/shard_map/ppermute | solution.py:43
  97.2 25.1 %collective-permute-start.9 = (bf16[8,2,128,128]{3,2,1,0:T(8,128)(2,1)S(1)}, bf16[8,2,128,128]{3,2,1,0:T(8,128)(2,1)S(1)}, u32[]{:S(2)}, u32[]{:S(2)}) collective-permute-start(bf16[8,2,128,128]{3,2,1,0:T(8,128)(2,1)S(1)} %copy-done.6), channel_id=1, source_target_pairs={{8,9},{24,25},{13,12},{29,28},{10,11},{26,27},{15,14},{31,30}} | collective-permute-start | bytes 1572872 | tf_op jit(solution)/shard_map/ppermute | solution.py:43
  102.5 28.1 %collective-permute-start.11 = (bf16[8,2,128,128]{3,2,1,0:T(8,128)(2,1)}, bf16[8,2,128,128]{3,2,1,0:T(8,128)(2,1)S(1)}, u32[]{:S(2)}, u32[]{:S(2)}) collective-permute-start(bf16[8,2,128,128]{3,2,1,0:T(8,128)(2,1)} %get-tuple-element.23), channel_id=1, source_target_pairs={{0,1},{16,17},{5,4},{21,20},{2,3},{18,19},{7,6},{23,22}} | collective-permute-start | bytes 1572872 | tf_op jit(solution)/shard_map/ppermute | solution.py:43
  103.8 38.0 %collective-permute-start.20 = (bf16[8,2,128,128]{3,2,1,0:T(8,128)(2,1)}, bf16[8,2,128,128]{3,2,1,0:T(8,128)(2,1)S(1)}, u32[]{:S(2)}, u32[]{:S(2)}) collective-permute-start(bf16[8,2,128,128]{3,2,1,0:T(8,128)(2,1)} %get-tuple-element.30), channel_id=1, source_target_pairs={{0,1},{4,5},{8,9},{12,13},{16,17},{20,21},{24,25},{28,29},{1,0},{5... | collective-permute-start | bytes 1572872 | tf_op jit(solution)/shard_map/ppermute | solution.py:43
  110.4 31.5 %collective-permute-start.21 = (bf16[8,2,128,128]{3,2,1,0:T(8,128)(2,1)}, bf16[8,2,128,128]{3,2,1,0:T(8,128)(2,1)}, u32[]{:S(2)}, u32[]{:S(2)}) collective-permute-start(bf16[8,2,128,128]{3,2,1,0:T(8,128)(2,1)} %get-tuple-element.31), channel_id=1, source_target_pairs={{8,9},{24,25},{13,12},{29,28},{10,11},{26,27},{15,14},{31,30}} | collective-permute-start | bytes 1572872 | tf_op jit(solution)/shard_map/ppermute | solution.py:43
  120.1 28.5 %collective-permute-start.22 = (bf16[8,2,128,128]{3,2,1,0:T(8,128)(2,1)}, bf16[8,2,128,128]{3,2,1,0:T(8,128)(2,1)S(1)}, u32[]{:S(2)}, u32[]{:S(2)}) collective-permute-start(bf16[8,2,128,128]{3,2,1,0:T(8,128)(2,1)} %get-tuple-element.32), channel_id=1, source_target_pairs={{0,1},{4,5},{8,9},{12,13},{16,17},{20,21},{24,25},{28,29},{1,0},{5... | collective-permute-start | bytes 1572872 | tf_op jit(solution)/shard_map/ppermute | solution.py:43
  122.3 32.1 %collective-permute-start.23 = (bf16[8,2,128,128]{3,2,1,0:T(8,128)(2,1)}, bf16[8,2,128,128]{3,2,1,0:T(8,128)(2,1)}, u32[]{:S(2)}, u32[]{:S(2)}) collective-permute-start(bf16[8,2,128,128]{3,2,1,0:T(8,128)(2,1)} %get-tuple-element.33), channel_id=1, source_target_pairs={{0,1},{16,17},{5,4},{21,20},{2,3},{18,19},{7,6},{23,22}} | collective-permute-start | bytes 1572872 | tf_op jit(solution)/shard_map/ppermute | solution.py:43
  (2 other events, 1.6 us)
where the time goes:
time: 157 us
  waiting for transfers between devices  83.2 us (53%)
  starting transfers between devices  37.4 us (24%)
  Pallas kernels  27.9 us (18%)
  local copies, waits for them, and re-layouts  6.68 us (4%)
    ppermute x24, waiting for transfers between devices, permute(): return lax.ppermute(block, ('rows', 'rep'), pairs)  83.2 us
    ppermute x24, starting transfers between devices, permute(): return lax.ppermute(block, ('rows', 'rep'), pairs)  37.4 us
    pallas_call x4, Pallas kernels, product(): pl.pallas_call(functools.partial(product_kernel, first, full is not None)...  20.9 us
    pallas_call x4, Pallas kernels, place(): pl.pallas_call(place_kernel, out_shape=jax.ShapeDtypeStruct(full.shape, f...  6.98 us
  transfers between devices with their start and end apart: 24, of which 10 were waited for; matrix products, arithmetic and copies ran while one was open for 1% of the time, Pallas kernels for 16%

commit v1 on v0

v1 whole, which is shorter than its diff:
```python
import functools

import jax
import jax.numpy as jnp
from jax import lax
from jax.experimental import pallas as pl
from jax.experimental.pallas import tpu as pltpu
from jax.sharding import PartitionSpec as P


HALF = 2
KP = 2
CLASSES = 2 * HALF

COST = 2**20
VMEM_LIMIT = 16 * 2**20


def down_offset(panel, kind):
    return (kind - panel + HALF) % CLASSES - HALF


def up_offset(panel, kind):
    return (kind - panel + HALF - 1) % CLASSES - HALF + 1


def classes_of(rep):
    return (rep % 2, rep % 2 + 2)


def route(panels, reps, target, kept=lambda panel, rep: True):
    pairs = []
    for rep in range(reps):
        for panel in range(panels):
            to_panel, to_rep = target(panel, rep)
            to_panel %= panels
            if kept(to_panel, to_rep):
                pairs.append((panel * reps + rep, to_panel * reps + to_rep))
    return pairs


def permute(block, pairs):
    return lax.ppermute(block, ("rows", "rep"), pairs)


def tile_table(pattern, device, blocks):
    count = pattern.shape[1]
    unit = blocks * KP
    even = device % 2 == 0
    mine = lax.dynamic_slice_in_dim(pattern, device * blocks, blocks, 0)
    rows = jnp.take(pattern, mine, axis=0, mode="clip")
    same = rows[:, :, :, None] == mine[:, None, None, :]
    slots = jnp.arange(count, dtype=jnp.int32)
    found = jnp.max(jnp.where(same, slots[None, None, :, None], -1), axis=2)
    offset = slots // KP - HALF
    turned = jnp.where(even, offset, -offset)
    far = jnp.where(turned == 1, 2, jnp.where(turned == -1, 3, jnp.where(turned == -HALF, 4, 5)))
    own = jnp.where((offset == HALF) == even, 0, 1)
    region = jnp.where(offset[:, None] == 0, own[None, :], far[:, None])
    place = region[None] * unit + (mine % blocks)[:, :, None] * KP + found % KP
    return jnp.where(found >= 0, place, 6 * unit).reshape(-1)


def row_product(left, right, table, i, slot, begin, end):
    count = left.shape[1]
    lefts = jnp.concatenate([left[i, s] for s in range(begin, end)], axis=1)
    rights = jnp.concatenate(
        [
            jnp.concatenate(
                [right[table[(i * count + s) * count + slot + e]] for e in range(KP)], axis=1
            )
            for s in range(begin, end)
        ],
        axis=0,
    )
    return jnp.dot(lefts, rights, preferred_element_type=jnp.float32)


def low_slot(offset):
    return pl.multiple_of((offset + HALF) * KP, KP)


def first_kernel(aliased, facts, table, coeffs, left_hbm, *refs):
    sources, refs = refs[:6], refs[6 + aliased :]
    full, main, extra, send0, send1, left, right, sums, baby, left_sems, in_sems, out_sem = refs
    blocks, count, tile = left.shape[0], left.shape[1], left.shape[2]
    unit = blocks * KP
    high = 2 * HALF * KP
    loads = [
        pltpu.make_async_copy(source, right.at[pl.ds(k * unit, unit)], in_sems.at[k])
        for k, source in enumerate(sources)
    ]

    def left_load(i):
        return pltpu.make_async_copy(left_hbm.at[i], left.at[i], left_sems.at[i])

    for load in loads:
        load.start()
    for i in range(blocks):
        left_load(i).start()
    right[6 * unit] = jnp.zeros((tile, tile), right.dtype)
    offset = facts[0]
    even = facts[1] == 1
    both = offset == -HALF
    for load in loads:
        load.wait()

    def put(source, target):
        return pltpu.make_async_copy(source, target, out_sem)

    def one_unit(which, slot, begin, end):
        def one_row(i, carry):
            if which == 0:
                left_load(i).wait()
            total = row_product(left, right, table, i, slot, begin, end)
            rounded = total.astype(jnp.bfloat16)
            for e in range(KP):
                part = rounded[:, e * tile : (e + 1) * tile]
                sums[which, i, e] = part
                mixed = coeffs[1] * left[i, slot + e].astype(jnp.float32) + coeffs[2] * part.astype(
                    jnp.float32
                )
                if slot + e == HALF * KP:
                    line = lax.broadcasted_iota(jnp.int32, (tile, tile), 0)
                    column = lax.broadcasted_iota(jnp.int32, (tile, tile), 1)
                    mixed = jnp.where(line == column, coeffs[0], 0.0) + mixed
                baby[which, i, e] = mixed.astype(jnp.bfloat16)
            put(sums.at[which, i], full.at[i, pl.ds(slot, KP)]).start()
            put(sums.at[which, i], (extra if which else main).at[i]).start()
            if begin == 0 and slot == 0 or which:
                @pl.when(even if which else jnp.logical_not(even))
                def _():
                    put(baby.at[which, i], send0.at[i]).start()

                @pl.when(jnp.logical_not(even) if which else even)
                def _():
                    put(baby.at[which, i], send1.at[i]).start()
            else:
                put(baby.at[which, i], send0.at[i]).start()
                put(baby.at[which, i], send1.at[i]).start()
            return carry

        lax.fori_loop(0, blocks, one_row, 0)

    for o in range(-HALF, HALF):

        @pl.when(offset == o)
        def _(o=o):
            begin = max(0, o) * KP
            end = (2 * HALF + 1 + min(0, o)) * KP
            one_unit(0, (o + HALF) * KP, begin, end)
            if o == -HALF:
                one_unit(1, high, HALF * KP, count)

    put(sums.at[0], main).wait()
    put(sums.at[0], full.at[:, pl.ds(low_slot(offset), KP)]).wait()
    put(baby.at[0], send0).wait()
    put(baby.at[0], send1).wait()

    @pl.when(both)
    def _():
        put(sums.at[1], extra).wait()
        put(sums.at[1], full.at[:, pl.ds(high, KP)]).wait()


SMEM_SPEC = pl.BlockSpec(memory_space=pltpu.SMEM)
ANY_SPEC = pl.BlockSpec(memory_space=pl.ANY)
HBM_SPEC = pl.BlockSpec(memory_space=pltpu.HBM)


def call(kernel, operands, scalars, outs, scratch, full_at=None, space=ANY_SPEC):
    return pl.pallas_call(
        kernel,
        out_shape=outs,
        in_specs=[SMEM_SPEC] * scalars + [space] * (len(operands) - scalars),
        out_specs=[HBM_SPEC] * len(outs),
        scratch_shapes=scratch,
        input_output_aliases={} if full_at is None else {full_at: 0},
        compiler_params=pltpu.CompilerParams(vmem_limit_bytes=VMEM_LIMIT),
        cost_estimate=pl.CostEstimate(flops=COST, bytes_accessed=2**23, transcendentals=0),
    )(*operands)


def units_of(blocks, tile, dtype):
    return jax.ShapeDtypeStruct((blocks, KP, tile, tile), dtype)


def first_product(facts, table, coeffs, left, rights, full):
    blocks, tile = left.shape[0], left.shape[2]
    unit = blocks * KP
    flat = [r.reshape(unit, tile, tile) for r in rights]
    operands = [facts, table, coeffs, left] + flat + ([] if full is None else [full])
    pair = pltpu.VMEM((2, blocks, KP, tile, tile), left.dtype)
    return call(
        functools.partial(first_kernel, full is not None),
        operands,
        3,
        [jax.ShapeDtypeStruct(left.shape, left.dtype)] + [units_of(blocks, tile, left.dtype)] * 4,
        [
            pltpu.VMEM(left.shape, left.dtype),
            pltpu.VMEM((6 * unit + 1, tile, tile), left.dtype),
            pair,
            pair,
            pltpu.SemaphoreType.DMA((blocks,)),
            pltpu.SemaphoreType.DMA((6,)),
            pltpu.SemaphoreType.DMA,
        ],
        None if full is None else len(operands) - 1,
    )


EARLY_REGIONS = (0, 1, 2, 3, 5)


def early_kernel(aliased, facts, table, left_hbm, *refs):
    sources, refs = refs[:5], refs[5 + aliased :]
    full, extra, partial, left, right, sums, totals, left_sems, in_sems, out_sem = refs
    blocks, count, tile = left.shape[0], left.shape[1], left.shape[2]
    unit = blocks * KP
    high = 2 * HALF * KP
    loads = [
        pltpu.make_async_copy(source, right.at[pl.ds(k * unit, unit)], in_sems.at[k])
        for k, source in zip(EARLY_REGIONS, sources)
    ]

    def left_load(i):
        return pltpu.make_async_copy(left_hbm.at[i], left.at[i], left_sems.at[i])

    for load in loads:
        load.start()
    for i in range(blocks):
        left_load(i).start()
    right[6 * unit] = jnp.zeros((tile, tile), right.dtype)
    offset = facts[0]
    even = facts[1] == 1
    both = offset == -HALF
    for load in loads:
        load.wait()

    def put(source, target):
        return pltpu.make_async_copy(source, target, out_sem)

    def whole_unit(slot, begin, end):
        def one_row(i, carry):
            left_load(i).wait()
            total = row_product(left, right, table, i, slot, begin, end)
            rounded = total.astype(jnp.bfloat16)
            for e in range(KP):
                sums[i, e] = rounded[:, e * tile : (e + 1) * tile]
            put(sums.at[i], full.at[i, pl.ds(slot, KP)]).start()
            put(sums.at[i], extra.at[i]).start()
            return carry

        lax.fori_loop(0, blocks, one_row, 0)

    def part_unit(loaded, slot, begin, end):
        def one_row(i, carry):
            if not loaded:
                left_load(i).wait()
            totals[i] = row_product(left, right, table, i, slot, begin, end)
            put(totals.at[i], partial.at[i]).start()
            return carry

        lax.fori_loop(0, blocks, one_row, 0)

    for parity in range(2):
        first, last = (KP, count) if parity == 0 else (0, count - KP)
        for o in range(-HALF, HALF):

            @pl.when(jnp.logical_and(offset == o, even if parity == 0 else jnp.logical_not(even)))
            def _(o=o, parity=parity, first=first, last=last):
                if o > -HALF:
                    begin = max(0, o) * KP
                    end = (2 * HALF + 1 + min(0, o)) * KP
                    part_unit(False, (o + HALF) * KP, max(begin, first), min(end, last))
                elif parity == 0:
                    whole_unit(high, HALF * KP, count)
                    part_unit(True, 0, first, (HALF + 1) * KP)
                else:
                    whole_unit(0, 0, (HALF + 1) * KP)
                    part_unit(True, high, HALF * KP, last)

    put(totals, partial).wait()

    @pl.when(both)
    def _():
        put(sums, extra).wait()
        put(sums, full.at[:, pl.ds(0, KP)]).wait()


def early_product(facts, table, left, rights, full):
    blocks, tile = left.shape[0], left.shape[2]
    unit = blocks * KP
    flat = [rights[k].reshape(unit, tile, tile) for k in EARLY_REGIONS]
    operands = [facts, table, left] + flat + ([] if full is None else [full])
    return call(
        functools.partial(early_kernel, full is not None),
        operands,
        2,
        [
            jax.ShapeDtypeStruct(left.shape, left.dtype),
            units_of(blocks, tile, left.dtype),
            jax.ShapeDtypeStruct((blocks, tile, KP * tile), jnp.float32),
        ],
        [
            pltpu.VMEM(left.shape, left.dtype),
            pltpu.VMEM((6 * unit + 1, tile, tile), left.dtype),
            pltpu.VMEM((blocks, KP, tile, tile), left.dtype),
            pltpu.VMEM((blocks, tile, KP * tile), jnp.float32),
            pltpu.SemaphoreType.DMA((blocks,)),
            pltpu.SemaphoreType.DMA((6,)),
            pltpu.SemaphoreType.DMA,
        ],
        None if full is None else len(operands) - 1,
    )


def late_kernel(facts, table, left_hbm, two, partial, full_in, full, main, *refs):
    del full_in
    left, right, sums, totals, in_sems, total_sems, out_sem = refs
    blocks, tile = left.shape[0], left.shape[2]
    count = left_hbm.shape[1]
    unit = blocks * KP
    offset = facts[0]
    even = facts[1] == 1
    both = offset == -HALF
    begin = jnp.where(even, 0, count - KP)
    slot = jnp.where(jnp.logical_and(both, jnp.logical_not(even)), 2 * HALF * KP, (offset + HALF) * KP)
    loads = [
        pltpu.make_async_copy(two, right.at[pl.ds(0, unit)], in_sems.at[0]),
        pltpu.make_async_copy(left_hbm.at[:, pl.ds(begin, KP)], left, in_sems.at[1]),
    ]

    def total_load(i):
        return pltpu.make_async_copy(partial.at[i], totals.at[i], total_sems.at[i])

    def put(source, target):
        return pltpu.make_async_copy(source, target, out_sem)

    for load in loads:
        load.start()
    for i in range(blocks):
        total_load(i).start()
    right[unit] = jnp.zeros((tile, tile), right.dtype)
    for load in loads:
        load.wait()

    def one_row(i, carry):
        total_load(i).wait()
        lefts = jnp.concatenate([left[i, s] for s in range(KP)], axis=1)
        rights = jnp.concatenate(
            [
                jnp.concatenate(
                    [
                        right[jnp.minimum(table[(i * count + begin + s) * count + slot + e] - 4 * unit, unit)]
                        for e in range(KP)
                    ],
                    axis=1,
                )
                for s in range(KP)
            ],
            axis=0,
        )
        total = totals[i] + jnp.dot(lefts, rights, preferred_element_type=jnp.float32)
        rounded = total.astype(jnp.bfloat16)
        for e in range(KP):
            sums[i, e] = rounded[:, e * tile : (e + 1) * tile]
        put(sums.at[i], main.at[i]).start()
        put(sums.at[i], full.at[i, pl.ds(slot, KP)]).start()
        return carry

    lax.fori_loop(0, blocks, one_row, 0)
    put(sums, main).wait()
    put(sums, full.at[:, pl.ds(slot, KP)]).wait()


def late_product(facts, table, left, two, partial, full):
    blocks, tile = left.shape[0], left.shape[2]
    unit = blocks * KP
    return call(
        late_kernel,
        [facts, table, left, two.reshape(unit, tile, tile), partial, full],
        2,
        [jax.ShapeDtypeStruct(left.shape, left.dtype), units_of(blocks, tile, left.dtype)],
        [
            pltpu.VMEM((blocks, KP, tile, tile), left.dtype),
            pltpu.VMEM((unit + 1, tile, tile), left.dtype),
            pltpu.VMEM((blocks, KP, tile, tile), left.dtype),
            pltpu.VMEM((blocks, tile, KP * tile), jnp.float32),
            pltpu.SemaphoreType.DMA((2,)),
            pltpu.SemaphoreType.DMA((blocks,)),
            pltpu.SemaphoreType.DMA,
        ],
        5,
    )


PIECES = 4


def place_kernel(number, facts, full_in, *refs):
    del full_in
    parts, (full, held, load_sems, store_sems) = refs[:number], refs[number:]
    rows = held.shape[1] // PIECES

    def load(k, piece):
        where = pl.ds(piece * rows, rows)
        return pltpu.make_async_copy(parts[k].at[where], held.at[k, where], load_sems.at[k, piece])

    def store(k, piece):
        where = pl.ds(piece * rows, rows)
        target = full.at[where, pl.ds(facts[2 * k], KP)]
        return pltpu.make_async_copy(held.at[k, where], target, store_sems.at[k, piece])

    def each(step):
        for k in range(number):

            @pl.when(facts[2 * k + 1] == 1)
            def _(k=k):
                for piece in range(PIECES):
                    step(k, piece)

    def move(k, piece):
        load(k, piece).wait()
        store(k, piece).start()

    each(lambda k, piece: load(k, piece).start())
    each(move)
    each(lambda k, piece: store(k, piece).wait())


def place(full, parts):
    number = len(parts)
    facts = jnp.stack([jnp.asarray(f, jnp.int32) for slot, counts, _ in parts for f in (slot, counts)])
    units = [unit for _, _, unit in parts]
    return call(
        functools.partial(place_kernel, number),
        [facts, full] + units,
        1,
        [jax.ShapeDtypeStruct(full.shape, full.dtype)],
        [
            pltpu.VMEM((number,) + units[0].shape, full.dtype),
            pltpu.SemaphoreType.DMA((number, PIECES)),
            pltpu.SemaphoreType.DMA((number, PIECES)),
        ],
        1,
    )[0]


def pick_kernel(slots, tiles, out0, out1, held, load_sems, store_sems):
    outs = (out0, out1)
    loads = [
        pltpu.make_async_copy(tiles.at[:, pl.ds(slots[k], KP)], held.at[k], load_sems.at[k])
        for k in range(2)
    ]
    stores = [pltpu.make_async_copy(held.at[k], outs[k], store_sems.at[k]) for k in range(2)]
    for load in loads:
        load.start()
    for load, store in zip(loads, stores):
        load.wait()
        store.start()
    for store in stores:
        store.wait()


def pick(tiles, slot0, slot1):
    blocks, tile = tiles.shape[0], tiles.shape[2]
    return call(
        pick_kernel,
        [jnp.stack([slot0, slot1]).astype(jnp.int32), tiles],
        1,
        [units_of(blocks, tile, tiles.dtype)] * 2,
        [
            pltpu.VMEM((2, blocks, KP, tile, tile), tiles.dtype),
            pltpu.SemaphoreType.DMA((2,)),
            pltpu.SemaphoreType.DMA((2,)),
        ],
        space=HBM_SPEC,
    )


def local(x_tiles, giant_tiles, coeffs, pattern):
    blocks = x_tiles.shape[0]
    panels = lax.axis_size("rows")
    reps = lax.axis_size("rep")
    device = lax.axis_index("rows")
    rep = lax.axis_index("rep")
    even = device % 2 == 0

    def swapped(panel):
        return panel + 1 if panel % 2 == 0 else panel - 1

    core_route = route(panels, reps, lambda p, z: (swapped(p), z))
    near_route = route(panels, reps, lambda p, z: (p - 1 if p % 2 == 0 else p + 1, z))

    def two_route(chunk):
        return route(
            panels,
            reps,
            lambda p, z: (p + 2 if p % 2 == 0 else p - 2, z),
            lambda p, z: (classes_of(z)[chunk] - p) % CLASSES != (1 if p % 2 == 0 else 3),
        )

    partner_route = route(panels, reps, lambda p, z: (p, z ^ 1))

    def extra_route(chunk):
        return route(
            panels,
            reps,
            lambda p, z: (p, z ^ 1),
            lambda p, z: down_offset(p, classes_of(z ^ 1)[chunk]) == -HALF,
        )

    def gathered(chunk, send0, send1):
        near = permute(send1, near_route)
        two = permute(send0, two_route(chunk))
        core = permute(send0, core_route)
        forwarded = permute(near, core_route)
        return (send0, send1, core, near, two, forwarded)

    def swapped_parts(chunk, main, extra):
        main = permute(main, partner_route)
        extra = permute(extra, extra_route(chunk))
        return main, extra

    def facts_of(kind):
        return jnp.stack([down_offset(device, kind), even.astype(jnp.int32)]).astype(jnp.int32)

    kinds = classes_of(rep)
    others = classes_of(1 - rep % 2)
    rights = []
    for chunk in range(2):
        up = (up_offset(device, kinds[chunk]) + HALF) * KP
        down = (down_offset(device, kinds[chunk]) + HALF) * KP
        send0, send1 = pick(x_tiles, jnp.where(even, up, down), jnp.where(even, down, up))
        rights.append(gathered(chunk, send0, send1))
    table = tile_table(pattern, device, blocks)
    unit = blocks * KP
    early_table = jnp.where(table // unit == 4, 6 * unit, table)

    squared = None
    babies = []
    parts = []
    top = 2 * HALF * KP
    for chunk in range(2):
        squared, main, extra, send0, send1 = first_product(
            facts_of(kinds[chunk]), table, coeffs, x_tiles, rights[chunk], squared
        )
        babies.append(gathered(chunk, send0, send1))
        main, extra = swapped_parts(chunk, main, extra)
        low = (down_offset(device, others[chunk]) + HALF) * KP
        parts += [(low, 1, main), (top, low == 0, extra)]
    squared = place(squared, parts)

    result = None
    parts = []
    for chunk in range(2):
        facts = facts_of(kinds[chunk])
        result, extra, partial = early_product(
            facts, early_table, giant_tiles, babies[chunk], result
        )
        result, main = late_product(facts, table, giant_tiles, babies[chunk][4], partial, result)
        main, extra = swapped_parts(chunk, main, extra)
        low = (down_offset(device, others[chunk]) + HALF) * KP
        both = low == 0
        late = jnp.where(both & ~even, top, low)
        parts += [(jnp.where(even, top, 0), both, extra), (late, 1, main)]
    result = place(result, parts[:-1])
    result = place(result, parts[-1:])
    return (squared, result)


def solution(mesh):
    return jax.shard_map(
        local,
        mesh=mesh,
        in_specs=(P("rows", None, None, None), P("rows", None, None, None), P(), P()),
        out_specs=(P("rows", None, None, None), P("rows", None, None, None)),
        check_vma=False,
    )
```

time: 157 us -> 145 us (0.924)
  waiting for transfers between devices: 83.2 us -> 60 us
  Pallas kernels: 27.9 us -> 44.2 us
  starting transfers between devices: 37.4 us -> 33.2 us
  local copies, waits for them, and re-layouts: 6.68 us -> 4.92 us
    ppermute x24, waiting for transfers between devices: 83.2 us -> 60 us  [permute(): return lax.ppermute(block, ('rows', 'rep'), pairs)]
    pallas_call x8 -> x11, Pallas kernels: 27.9 us -> 44.2 us  [call(): pl.pallas_call(kernel, out_shape=outs, in_specs=[SMEM_SPEC] * scalars + [...]
    ppermute x24, starting transfers between devices: 37.4 us -> 33.2 us  [permute(): return lax.ppermute(block, ('rows', 'rep'), pairs)]
    dynamic_slice x1 -> x0, local copies, waits for them, and re-layouts: 2.87 us -> none  [local(): send1 = lax.dynamic_slice_in_dim(x_tiles, jnp.where(even, down, up), KP, 1)]
    unnamed x21 -> x19, local copies, waits for them, and re-layouts: 2.52 us -> 3.46 us
  transfers between devices with their start and end apart: 24 -> 24, of which waited for: 10 -> 7; matrix products, arithmetic and copies ran while one was open for 1% -> 2% of each run, Pallas kernels for 16% -> 28%
where the time goes in v1:
time: 145 us; the launch traced here: 144 us
  waiting for transfers between devices  60 us (41%)
  Pallas kernels  44.2 us (30%)
  starting transfers between devices  33.2 us (23%)
  local copies, waits for them, and re-layouts  4.92 us (3%)
    ppermute x24, waiting for transfers between devices, permute(): return lax.ppermute(block, ('rows', 'rep'), pairs)  60 us
    pallas_call x11, Pallas kernels, call(): pl.pallas_call(kernel, out_shape=outs, in_specs=[SMEM_SPEC] * scalars + [...  44.2 us
    ppermute x24, starting transfers between devices, permute(): return lax.ppermute(block, ('rows', 'rep'), pairs)  33.2 us
    unnamed x19, local copies, waits for them, and re-layouts  3.46 us
  transfers between devices with their start and end apart: 24, of which 7 were waited for; matrix products, arithmetic and copies ran while one was open for 2% of the time, Pallas kernels for 28%

profile of v1, /device:TPU:1, one launch (start us, length us, event | category | flops | bytes accessed | tf_op | source)
XLA Modules:
  0.0 144.1 jit_solution(2123561808165807899)
XLA Ops:
  0.8 1.7 %copy-done = bf16[8,10,128,128]{3,2,1,0:T(8,128)(2,1)S(1)} copy-done((bf16[8,10,128,128]{3,2,1,0:T(8,128)(2,1)S(1)}, bf16[8,10,128,128]{3,2,1,0:T(8,128)(2,1)}, u32[]{:S(2)}) %copy-start) | copy-done | bytes 2621464
  2.5 1.7 %shard_map.60 = (bf16[8,2,128,128]{3,2,1,0:T(8,128)(2,1)}, bf16[8,2,128,128]{3,2,1,0:T(8,128)(2,1)}) custom-call(s32[2]{0:T(128)S(1)} %pad_add_fusion.3.slots, bf16[8,10,128,128]{3,2,1,0:T(8,128)(2,1)S(1)} %copy-done), custom_call_target="tpu_custom_call" | custom-call | flops 1048576 | bytes 8388608 | tf_op jit(solution)/shard_map/pallas_call | solution.py:172
  4.2 5.7 %collective-permute-start.6 = (bf16[8,2,128,128]{3,2,1,0:T(8,128)(2,1)}, bf16[8,2,128,128]{3,2,1,0:T(8,128)(2,1)}, u32[]{:S(2)}, u32[]{:S(2)}) collective-permute-start(bf16[8,2,128,128]{3,2,1,0:T(8,128)(2,1)} %get-tuple-element.28), channel_id=1, source_target_pairs={{0,8},{4,28},{8,16},{16,24},{20,12},{24,0},{1,9},{5,29},{13,5},{17... | collective-permute-start | bytes 1572872 | tf_op jit(solution)/shard_map/ppermute | solution.py:43
  10.4 1.5 %shard_map.59 = (bf16[8,2,128,128]{3,2,1,0:T(8,128)(2,1)S(1)}, bf16[8,2,128,128]{3,2,1,0:T(8,128)(2,1)}) custom-call(s32[2]{0:T(128)S(1)} %pad_add_fusion.1.slots, bf16[8,10,128,128]{3,2,1,0:T(8,128)(2,1)S(1)} %copy-done.1), custom_call_target="tpu_custom_call" | custom-call | flops 1048576 | bytes 8388608 | tf_op jit(solution)/shard_map/pallas_call | solution.py:172
  11.9 1.3 collective-permute-start.1
  13.2 1.3 collective-permute-start.2
  16.1 17.1 %collective-permute-done.5 = bf16[8,2,128,128]{3,2,1,0:T(8,128)(2,1)} collective-permute-done((bf16[8,2,128,128]{3,2,1,0:T(8,128)(2,1)}, bf16[8,2,128,128]{3,2,1,0:T(8,128)(2,1)}, u32[]{:S(2)}, u32[]{:S(2)}) %collective-permute-start.5) | collective-permute-done | bytes 524320 | tf_op jit(solution)/shard_map/ppermute | solution.py:43
  34.1 10.4 %collective-permute-done.1 = bf16[8,2,128,128]{3,2,1,0:T(8,128)(2,1)} collective-permute-done((bf16[8,2,128,128]{3,2,1,0:T(8,128)(2,1)}, bf16[8,2,128,128]{3,2,1,0:T(8,128)(2,1)}, u32[]{:S(2)}, u32[]{:S(2)}) %collective-permute-start.1) | collective-permute-done | bytes 524320 | tf_op jit(solution)/shard_map/ppermute | solution.py:43
  44.6 6.5 %shard_map.61 = (bf16[8,10,128,128]{3,2,1,0:T(8,128)(2,1)}, bf16[8,2,128,128]{3,2,1,0:T(8,128)(2,1)S(1)}, bf16[8,2,128,128]{3,2,1,0:T(8,128)(2,1)}, bf16[8,2,128...) custom-call(s32[2]{0:T(128)S(1)} %pad_add_fusion.2.facts, s32[800]{0:T(1024)S(1)} %get-tuple-element.51.table, ...), custom_call_target="tpu_custom_call" | custom-call | flops 1048576 | bytes 8388608 | tf_op jit(solution)/shard_map/pallas_call | solution.py:172
  52.7 3.2 %collective-permute-start.18 = (bf16[8,2,128,128]{3,2,1,0:T(8,128)(2,1)}, bf16[8,2,128,128]{3,2,1,0:T(8,128)(2,1)}, u32[]{:S(2)}, u32[]{:S(2)}) collective-permute-start(bf16[8,2,128,128]{3,2,1,0:T(8,128)(2,1)} %get-tuple-element.39), channel_id=1, source_target_pairs={{0,28},{4,8},{8,4},{12,16},{16,12},{20,24},{24,20},{28,0},{1,29},{... | collective-permute-start | bytes 1572872 | tf_op jit(solution)/shard_map/ppermute | solution.py:43
  56.0 7.2 %shard_map.62 = (bf16[8,10,128,128]{3,2,1,0:T(8,128)(2,1)}, bf16[8,2,128,128]{3,2,1,0:T(8,128)(2,1)S(1)}, bf16[8,2,128,128]{3,2,1,0:T(8,128)(2,1)S(1)}, bf16[8,2...) custom-call(s32[2]{0:T(128)S(1)} %pad_add_fusion.facts, ...), custom_call_target="tpu_custom_call", output_to_operand_aliasing={{0}: (10, {})} | custom-call | flops 1048576 | bytes 8388608 | tf_op jit(solution)/shard_map/pallas_call | solution.py:172
  63.5 1.6 %collective-permute-start.13 = (bf16[8,2,128,128]{3,2,1,0:T(8,128)(2,1)S(1)}, bf16[8,2,128,128]{3,2,1,0:T(8,128)(2,1)S(1)}, u32[]{:S(2)}, u32[]{:S(2)}) collective-permute-start(bf16[8,2,128,128]{3,2,1,0:T(8,128)(2,1)S(1)} %get-tuple-element.36), channel_id=1, source_target_pairs={{0,4},{4,0},{8,12},{12,8},{16,20},{20,16},{24,28},{28,24},{1,5},{5... | collective-permute-start | bytes 1572872 | tf_op jit(solution)/shard_map/ppermute | solution.py:43
  65.2 4.5 %collective-permute-start.16 = (bf16[8,2,128,128]{3,2,1,0:T(8,128)(2,1)S(1)}, bf16[8,2,128,128]{3,2,1,0:T(8,128)(2,1)S(1)}, u32[]{:S(2)}, u32[]{:S(2)}) collective-permute-start(bf16[8,2,128,128]{3,2,1,0:T(8,128)(2,1)S(1)} %copy-done.4), channel_id=1, source_target_pairs={{0,8},{4,28},{8,16},{16,24},{20,12},{24,0},{1,9},{5,29},{13,5},{17... | collective-permute-start | bytes 1572872 | tf_op jit(solution)/shard_map/ppermute | solution.py:43
  69.8 9.3 %collective-permute-done.14 = bf16[8,2,128,128]{3,2,1,0:T(8,128)(2,1)S(1)} collective-permute-done((bf16[8,2,128,128]{3,2,1,0:T(8,128)(2,1)S(1)}, bf16[8,2,128,128]{3,2,1,0:T(8,128)(2,1)S(1)}, u32[]{:S(2)}, u32[]{:S(2)}) %collective-permute-start.14) | collective-permute-done | bytes 524320 | tf_op jit(solution)/shard_map/ppermute | solution.py:43
  79.1 1.0 collective-permute-start.15
  80.1 1.5 %collective-permute-start.10 = (bf16[8,2,128,128]{3,2,1,0:T(8,128)(2,1)S(1)}, bf16[8,2,128,128]{3,2,1,0:T(8,128)(2,1)S(1)}, u32[]{:S(2)}, u32[]{:S(2)}) collective-permute-start(bf16[8,2,128,128]{3,2,1,0:T(8,128)(2,1)S(1)} %get-tuple-element.34), channel_id=1, source_target_pairs={{0,1},{4,5},{8,9},{12,13},{16,17},{20,21},{24,25},{28,29},{1,0},{5... | collective-permute-start | bytes 1572872 | tf_op jit(solution)/shard_map/ppermute | solution.py:43
  81.6 1.3 collective-permute-start.11
  82.9 6.7 %collective-permute-done.16 = bf16[8,2,128,128]{3,2,1,0:T(8,128)(2,1)S(1)} collective-permute-done((bf16[8,2,128,128]{3,2,1,0:T(8,128)(2,1)S(1)}, bf16[8,2,128,128]{3,2,1,0:T(8,128)(2,1)S(1)}, u32[]{:S(2)}, u32[]{:S(2)}) %collective-permute-start.16) | collective-permute-done | bytes 524320 | tf_op jit(solution)/shard_map/ppermute | solution.py:43
  89.6 1.3 collective-permute-start.12
  90.9 3.3 %collective-permute-start.8 = (bf16[8,2,128,128]{3,2,1,0:T(8,128)(2,1)S(1)}, bf16[8,2,128,128]{3,2,1,0:T(8,128)(2,1)S(1)}, u32[]{:S(2)}, u32[]{:S(2)}) collective-permute-start(bf16[8,2,128,128]{3,2,1,0:T(8,128)(2,1)S(1)} %copy-done.7), channel_id=1, source_target_pairs={{0,1},{4,5},{8,9},{12,13},{16,17},{20,21},{24,25},{28,29},{1,0},{5... | collective-permute-start | bytes 1572872 | tf_op jit(solution)/shard_map/ppermute | solution.py:43
  94.3 5.3 %shard_map.64 = (bf16[8,10,128,128]{3,2,1,0:T(8,128)(2,1)}, bf16[8,2,128,128]{3,2,1,0:T(8,128)(2,1)}, f32[8,128,256]{2,1,0:T(8,128)S(1)}) custom-call(s32[2]{0:T(128)S(1)} %pad_add_fusion.2.facts, s32[800]{0:T(1024)S(1)} %get-tuple-element.50.table, bf16[8,10,128,128]{3,2,1,0:T(8,128)(2,1)S(1)} %copy-done.2, bf16[16,128,128]{2,1,0:T(8,128)(2,1)S(1)} %bitcast.42, ...), custom_call_target="tpu_custom_call" | custom-call | flops 1048576 | bytes 8388608 | tf_op jit(solution)/shard_map/pallas_call | solution.py:172
  99.6 4.2 %shard_map.65 = (bf16[8,10,128,128]{3,2,1,0:T(8,128)(2,1)}, bf16[8,2,128,128]{3,2,1,0:T(8,128)(2,1)}) custom-call(s32[2]{0:T(128)S(1)} %pad_add_fusion.2.facts, s32[800]{0:T(1024)S(1)} %get-tuple-element.51.table, bf16[8,10,128,128]{3,2,1,0:T(8,128)(2,1)S(1)} %copy-done.2, bf16[16,128,128]{2,1,0:T(8,128)(2,1)S(1)} %bitcast.48, ...), custom_call_target="tpu_custom_call", output_to_operand_aliasing={{0}: (5, {})} | custom-call | flops 1048576 | bytes 8388608 | tf_op jit(solution)/shard_map/pallas_call | solution.py:172
  104.5 4.9 %shard_map.66 = (bf16[8,10,128,128]{3,2,1,0:T(8,128)(2,1)}, bf16[8,2,128,128]{3,2,1,0:T(8,128)(2,1)}, f32[8,128,256]{2,1,0:T(8,128)S(1)}) custom-call(s32[2]{0:T(128)S(1)} %pad_add_fusion.facts, s32[800]{0:T(1024)S(1)} %get-tuple-element.50.table, bf16[8,10,128,128]{3,2,1,0:T(8,128)(2,1)S(1)} %copy-done.2, ...), custom_call_target="tpu_custom_call", output_to_operand_aliasing={{0}: (8, {})} | custom-call | flops 1048576 | bytes 8388608 | tf_op jit(solution)/shard_map/pallas_call | solution.py:172
  109.4 1.3 collective-permute-start.22
  110.7 2.2 %collective-permute-start.21 = (bf16[8,2,128,128]{3,2,1,0:T(8,128)(2,1)}, bf16[8,2,128,128]{3,2,1,0:T(8,128)(2,1)}, u32[]{:S(2)}, u32[]{:S(2)}) collective-permute-start(bf16[8,2,128,128]{3,2,1,0:T(8,128)(2,1)} %get-tuple-element.47), channel_id=1, source_target_pairs={{0,1},{4,5},{8,9},{12,13},{16,17},{20,21},{24,25},{28,29},{1,0},{5... | collective-permute-start | bytes 1572872 | tf_op jit(solution)/shard_map/ppermute | solution.py:43
  112.9 1.5 %collective-permute-start.20 = (bf16[8,2,128,128]{3,2,1,0:T(8,128)(2,1)}, bf16[8,2,128,128]{3,2,1,0:T(8,128)(2,1)}, u32[]{:S(2)}, u32[]{:S(2)}) collective-permute-start(bf16[8,2,128,128]{3,2,1,0:T(8,128)(2,1)} %get-tuple-element.46), channel_id=1, source_target_pairs={{8,9},{24,25},{13,12},{29,28},{10,11},{26,27},{15,14},{31,30}} | collective-permute-start | bytes 1572872 | tf_op jit(solution)/shard_map/ppermute | solution.py:43
  114.4 4.2 %shard_map.67 = (bf16[8,10,128,128]{3,2,1,0:T(8,128)(2,1)}, bf16[8,2,128,128]{3,2,1,0:T(8,128)(2,1)}) custom-call(s32[2]{0:T(128)S(1)} %pad_add_fusion.facts, s32[800]{0:T(1024)S(1)} %get-tuple-element.51.table, bf16[8,10,128,128]{3,2,1,0:T(8,128)(2,1)S(1)} %copy-done.2, bf16[16,128,128]{2,1,0:T(8,128)(2,1)S(1)} %bitcast.46, ...), custom_call_target="tpu_custom_call", output_to_operand_aliasing={{0}: (5, {})} | custom-call | flops 1048576 | bytes 8388608 | tf_op jit(solution)/shard_map/pallas_call | solution.py:172
  119.0 4.0 %shard_map.63 = bf16[8,10,128,128]{3,2,1,0:T(8,128)(2,1)} custom-call(s32[8]{0:T(128)S(1)} %stack.88.facts, bf16[8,10,128,128]{3,2,1,0:T(8,128)(2,1)} %get-tuple-element.31.full_in, bf16[8,2,128,128]{3,2,1,0:T(8,128)(2,1)S(1)} %collective-permute-done.8.refs_0_, ...), custom_call_target="tpu_custom_call", output_to_operand_aliasing={{}: (1, {})} | custom-call | flops 1048576 | bytes 8388608 | tf_op jit(solution)/shard_map/pallas_call | solution.py:172
  123.4 11.1 %collective-permute-done.21.refs_1_ = bf16[8,2,128,128]{3,2,1,0:T(8,128)(2,1)} collective-permute-done((bf16[8,2,128,128]{3,2,1,0:T(8,128)(2,1)}, bf16[8,2,128,128]{3,2,1,0:T(8,128)(2,1)}, u32[]{:S(2)}, u32[]{:S(2)}) %collective-permute-start.21) | collective-permute-done | bytes 524320 | tf_op jit(solution)/shard_map/ppermute | solution.py:43
  134.5 2.7 %shard_map.68.full_in = bf16[8,10,128,128]{3,2,1,0:T(8,128)(2,1)} custom-call(s32[6]{0:T(128)S(1)} %stack.105.facts, bf16[8,10,128,128]{3,2,1,0:T(8,128)(2,1)} %get-tuple-element.45.full_in, bf16[8,2,128,128]{3,2,1,0:T(8,128)(2,1)} %collective-permute-done.20.refs_0_, ...), custom_call_target="tpu_custom_call", output_to_operand_aliasing={{}: (1, {})} | custom-call | flops 1048576 | bytes 8388608 | tf_op jit(solution)/shard_map/pallas_call | solution.py:172
  137.2 4.8 %collective-permute-done.23.refs_0_ = bf16[8,2,128,128]{3,2,1,0:T(8,128)(2,1)S(1)} collective-permute-done((bf16[8,2,128,128]{3,2,1,0:T(8,128)(2,1)}, bf16[8,2,128,128]{3,2,1,0:T(8,128)(2,1)S(1)}, u32[]{:S(2)}, u32[]{:S(2)}) %collective-permute-start.23) | collective-permute-done | bytes 524320 | tf_op jit(solution)/shard_map/ppermute | solution.py:43
  142.0 2.1 %shard_map.69 = bf16[8,10,128,128]{3,2,1,0:T(8,128)(2,1)} custom-call(s32[2]{0:T(128)S(1)} %pad_add_fusion.4.facts, bf16[8,10,128,128]{3,2,1,0:T(8,128)(2,1)} %shard_map.68.full_in, bf16[8,2,128,128]{3,2,1,0:T(8,128)(2,1)S(1)} %collective-permute-done.23.refs_0_), custom_call_target="tpu_custom_call", output_to_operand_aliasing={{}: (1, {})} | custom-call | flops 1048576 | bytes 8388608 | tf_op jit(solution)/shard_map/pallas_call | solution.py:172
  (69 shorter events, 6.7 us)
Async XLA Ops:
  0.8 1.7 %copy-start = (bf16[8,10,128,128]{3,2,1,0:T(8,128)(2,1)S(1)}, bf16[8,10,128,128]{3,2,1,0:T(8,128)(2,1)}, u32[]{:S(2)}) copy-start(bf16[8,10,128,128]{3,2,1,0:T(8,128)(2,1)} %left_hbm.7) | copy-start | bytes 7864324
  2.5 7.9 %copy-start.1 = (bf16[8,10,128,128]{3,2,1,0:T(8,128)(2,1)S(1)}, bf16[8,10,128,128]{3,2,1,0:T(8,128)(2,1)}, u32[]{:S(2)}) copy-start(bf16[8,10,128,128]{3,2,1,0:T(8,128)(2,1)} %left_hbm.7) | copy-start | bytes 7864324
  2.5 12.0 %copy-start.8 = (s32[64,10]{0,1:T(8,128)S(1)}, s32[64,10]{0,1:T(8,128)}, u32[]{:S(2)}) copy-start(s32[64,10]{0,1:T(8,128)} %param.7) | copy-start | bytes 7684
  4.2 40.4 %copy-start.5 = (f32[3]{0:T(128)S(1)}, f32[3]{0:T(128)}, u32[]{:S(2)}) copy-start(f32[3]{0:T(128)} %coeffs.3) | copy-start | bytes 40
  4.2 29.3 %collective-permute-start.6 = (bf16[8,2,128,128]{3,2,1,0:T(8,128)(2,1)}, bf16[8,2,128,128]{3,2,1,0:T(8,128)(2,1)}, u32[]{:S(2)}, u32[]{:S(2)}) collective-permute-start(bf16[8,2,128,128]{3,2,1,0:T(8,128)(2,1)} %get-tuple-element.28), channel_id=1, source_target_pairs={{0,8},{4,28},{8,16},{16,24},{20,12},{24,0},{1,9},{5,29},{13,5},{17... | collective-permute-start | bytes 1572872 | tf_op jit(solution)/shard_map/ppermute | solution.py:43
  9.9 34.7 %collective-permute-start.4 = (bf16[8,2,128,128]{3,2,1,0:T(8,128)(2,1)}, bf16[8,2,128,128]{3,2,1,0:T(8,128)(2,1)}, u32[]{:S(2)}, u32[]{:S(2)}) collective-permute-start(bf16[8,2,128,128]{3,2,1,0:T(8,128)(2,1)} %get-tuple-element.28), channel_id=1, source_target_pairs={{0,4},{4,0},{8,12},{12,8},{16,20},{20,16},{24,28},{28,24},{1,5},{5... | collective-permute-start | bytes 1572872 | tf_op jit(solution)/shard_map/ppermute | solution.py:43
  9.9 23.4 %collective-permute-start.5 = (bf16[8,2,128,128]{3,2,1,0:T(8,128)(2,1)}, bf16[8,2,128,128]{3,2,1,0:T(8,128)(2,1)}, u32[]{:S(2)}, u32[]{:S(2)}) collective-permute-start(bf16[8,2,128,128]{3,2,1,0:T(8,128)(2,1)} %get-tuple-element.29), channel_id=1, source_target_pairs={{0,28},{4,8},{8,4},{12,16},{16,12},{20,24},{24,20},{28,0},{1,29},{... | collective-permute-start | bytes 1572872 | tf_op jit(solution)/shard_map/ppermute | solution.py:43
  11.9 32.6 %collective-permute-start.1 = (bf16[8,2,128,128]{3,2,1,0:T(8,128)(2,1)}, bf16[8,2,128,128]{3,2,1,0:T(8,128)(2,1)}, u32[]{:S(2)}, u32[]{:S(2)}) collective-permute-start(bf16[8,2,128,128]{3,2,1,0:T(8,128)(2,1)} %get-tuple-element.27), channel_id=1, source_target_pairs={{0,28},{4,8},{8,4},{12,16},{16,12},{20,24},{24,20},{28,0},{1,29},{... | collective-permute-start | bytes 1572872 | tf_op jit(solution)/shard_map/ppermute | solution.py:43
  13.2 42.7 %collective-permute-start.2 = (bf16[8,2,128,128]{3,2,1,0:T(8,128)(2,1)S(1)}, bf16[8,2,128,128]{3,2,1,0:T(8,128)(2,1)}, u32[]{:S(2)}, u32[]{:S(2)}) collective-permute-start(bf16[8,2,128,128]{3,2,1,0:T(8,128)(2,1)S(1)} %get-tuple-element.26), channel_id=1, source_target_pairs={{0,8},{8,16},{12,4},{16,24},{24,0},{28,20},{5,29},{9,17},{13,5},{2... | collective-permute-start | bytes 1572872 | tf_op jit(solution)/shard_map/ppermute | solution.py:43
  33.3 11.3 %collective-permute-start.7 = (bf16[8,2,128,128]{3,2,1,0:T(8,128)(2,1)}, bf16[8,2,128,128]{3,2,1,0:T(8,128)(2,1)}, u32[]{:S(2)}, u32[]{:S(2)}) collective-permute-start(bf16[8,2,128,128]{3,2,1,0:T(8,128)(2,1)} %collective-permute-done.5), channel_id=1, source_target_pairs={{0,4},{4,0},{8,12},{12,8},{16,20},{20,16},{24,28},{28,24},{1,5},{5... | collective-permute-start | bytes 1572872 | tf_op jit(solution)/shard_map/ppermute | solution.py:43
  33.5 22.4 %collective-permute-start = (bf16[8,2,128,128]{3,2,1,0:T(8,128)(2,1)S(1)}, bf16[8,2,128,128]{3,2,1,0:T(8,128)(2,1)}, u32[]{:S(2)}, u32[]{:S(2)}) collective-permute-start(bf16[8,2,128,128]{3,2,1,0:T(8,128)(2,1)S(1)} %get-tuple-element.26), channel_id=1, source_target_pairs={{0,4},{4,0},{8,12},{12,8},{16,20},{20,16},{24,28},{28,24},{1,5},{5... | collective-permute-start | bytes 1572872 | tf_op jit(solution)/shard_map/ppermute | solution.py:43
  44.5 11.5 %collective-permute-start.3 = (bf16[8,2,128,128]{3,2,1,0:T(8,128)(2,1)}, bf16[8,2,128,128]{3,2,1,0:T(8,128)(2,1)}, u32[]{:S(2)}, u32[]{:S(2)}) collective-permute-start(bf16[8,2,128,128]{3,2,1,0:T(8,128)(2,1)} %collective-permute-done.1), channel_id=1, source_target_pairs={{0,4},{4,0},{8,12},{12,8},{16,20},{20,16},{24,28},{28,24},{1,5},{5... | collective-permute-start | bytes 1572872 | tf_op jit(solution)/shard_map/ppermute | solution.py:43
  51.9 0.8 copy-start.6
  52.7 17.0 %collective-permute-start.18 = (bf16[8,2,128,128]{3,2,1,0:T(8,128)(2,1)}, bf16[8,2,128,128]{3,2,1,0:T(8,128)(2,1)}, u32[]{:S(2)}, u32[]{:S(2)}) collective-permute-start(bf16[8,2,128,128]{3,2,1,0:T(8,128)(2,1)} %get-tuple-element.39), channel_id=1, source_target_pairs={{0,28},{4,8},{8,4},{12,16},{16,12},{20,24},{24,20},{28,0},{1,29},{... | collective-permute-start | bytes 1572872 | tf_op jit(solution)/shard_map/ppermute | solution.py:43
  56.0 9.1 %copy-start.4 = (bf16[8,2,128,128]{3,2,1,0:T(8,128)(2,1)S(1)}, bf16[8,2,128,128]{3,2,1,0:T(8,128)(2,1)}, u32[]{:S(2)}) copy-start(bf16[8,2,128,128]{3,2,1,0:T(8,128)(2,1)} %copy-done.3) | copy-start | bytes 1572868
  56.0 35.0 %copy-start.7 = (bf16[8,2,128,128]{3,2,1,0:T(8,128)(2,1)S(1)}, bf16[8,2,128,128]{3,2,1,0:T(8,128)(2,1)}, u32[]{:S(2)}) copy-start(bf16[8,2,128,128]{3,2,1,0:T(8,128)(2,1)} %copy-done.6) | copy-start | bytes 1572868
  56.0 38.3 %copy-start.2 = (bf16[8,10,128,128]{3,2,1,0:T(8,128)(2,1)S(1)}, bf16[8,10,128,128]{3,2,1,0:T(8,128)(2,1)}, u32[]{:S(2)}) copy-start(bf16[8,10,128,128]{3,2,1,0:T(8,128)(2,1)} %left_hbm.11) | copy-start | bytes 7864324
  63.2 15.9 %collective-permute-start.14 = (bf16[8,2,128,128]{3,2,1,0:T(8,128)(2,1)S(1)}, bf16[8,2,128,128]{3,2,1,0:T(8,128)(2,1)S(1)}, u32[]{:S(2)}, u32[]{:S(2)}) collective-permute-start(bf16[8,2,128,128]{3,2,1,0:T(8,128)(2,1)S(1)} %get-tuple-element.37), channel_id=1, source_target_pairs={{0,28},{4,8},{8,4},{12,16},{16,12},{20,24},{24,20},{28,0},{1,29},{... | collective-permute-start | bytes 1572872 | tf_op jit(solution)/shard_map/ppermute | solution.py:43
  63.5 16.6 %collective-permute-start.13 = (bf16[8,2,128,128]{3,2,1,0:T(8,128)(2,1)S(1)}, bf16[8,2,128,128]{3,2,1,0:T(8,128)(2,1)S(1)}, u32[]{:S(2)}, u32[]{:S(2)}) collective-permute-start(bf16[8,2,128,128]{3,2,1,0:T(8,128)(2,1)S(1)} %get-tuple-element.36), channel_id=1, source_target_pairs={{0,4},{4,0},{8,12},{12,8},{16,20},{20,16},{24,28},{28,24},{1,5},{5... | collective-permute-start | bytes 1572872 | tf_op jit(solution)/shard_map/ppermute | solution.py:43
  65.1 16.5 %collective-permute-start.17 = (bf16[8,2,128,128]{3,2,1,0:T(8,128)(2,1)S(1)}, bf16[8,2,128,128]{3,2,1,0:T(8,128)(2,1)S(1)}, u32[]{:S(2)}, u32[]{:S(2)}) collective-permute-start(bf16[8,2,128,128]{3,2,1,0:T(8,128)(2,1)S(1)} %copy-done.4), channel_id=1, source_target_pairs={{0,4},{4,0},{8,12},{12,8},{16,20},{20,16},{24,28},{28,24},{1,5},{5... | collective-permute-start | bytes 1572872 | tf_op jit(solution)/shard_map/ppermute | solution.py:43
  65.2 24.5 %collective-permute-start.16 = (bf16[8,2,128,128]{3,2,1,0:T(8,128)(2,1)S(1)}, bf16[8,2,128,128]{3,2,1,0:T(8,128)(2,1)S(1)}, u32[]{:S(2)}, u32[]{:S(2)}) collective-permute-start(bf16[8,2,128,128]{3,2,1,0:T(8,128)(2,1)S(1)} %copy-done.4), channel_id=1, source_target_pairs={{0,8},{4,28},{8,16},{16,24},{20,12},{24,0},{1,9},{5,29},{13,5},{17... | collective-permute-start | bytes 1572872 | tf_op jit(solution)/shard_map/ppermute | solution.py:43
  69.7 21.2 %collective-permute-start.19 = (bf16[8,2,128,128]{3,2,1,0:T(8,128)(2,1)}, bf16[8,2,128,128]{3,2,1,0:T(8,128)(2,1)S(1)}, u32[]{:S(2)}, u32[]{:S(2)}) collective-permute-start(bf16[8,2,128,128]{3,2,1,0:T(8,128)(2,1)} %collective-permute-done.18), channel_id=1, source_target_pairs={{0,4},{4,0},{8,12},{12,8},{16,20},{20,16},{24,28},{28,24},{1,5},{5... | collective-permute-start | bytes 1572872 | tf_op jit(solution)/shard_map/ppermute | solution.py:43
  79.1 24.7 %collective-permute-start.15 = (bf16[8,2,128,128]{3,2,1,0:T(8,128)(2,1)S(1)}, bf16[8,2,128,128]{3,2,1,0:T(8,128)(2,1)S(1)}, u32[]{:S(2)}, u32[]{:S(2)}) collective-permute-start(bf16[8,2,128,128]{3,2,1,0:T(8,128)(2,1)S(1)} %collective-permute-done.14), channel_id=1, source_target_pairs={{0,4},{4,0},{8,12},{12,8},{16,20},{20,16},{24,28},{28,24},{1,5},{5... | collective-permute-start | bytes 1572872 | tf_op jit(solution)/shard_map/ppermute | solution.py:43
  80.1 29.3 %collective-permute-start.10 = (bf16[8,2,128,128]{3,2,1,0:T(8,128)(2,1)S(1)}, bf16[8,2,128,128]{3,2,1,0:T(8,128)(2,1)S(1)}, u32[]{:S(2)}, u32[]{:S(2)}) collective-permute-start(bf16[8,2,128,128]{3,2,1,0:T(8,128)(2,1)S(1)} %get-tuple-element.34), channel_id=1, source_target_pairs={{0,1},{4,5},{8,9},{12,13},{16,17},{20,21},{24,25},{28,29},{1,0},{5... | collective-permute-start | bytes 1572872 | tf_op jit(solution)/shard_map/ppermute | solution.py:43
  81.6 29.1 %collective-permute-start.11 = (bf16[8,2,128,128]{3,2,1,0:T(8,128)(2,1)S(1)}, bf16[8,2,128,128]{3,2,1,0:T(8,128)(2,1)S(1)}, u32[]{:S(2)}, u32[]{:S(2)}) collective-permute-start(bf16[8,2,128,128]{3,2,1,0:T(8,128)(2,1)S(1)} %get-tuple-element.35), channel_id=1, source_target_pairs={{0,1},{16,17},{5,4},{21,20},{2,3},{18,19},{7,6},{23,22}} | collective-permute-start | bytes 1572872 | tf_op jit(solution)/shard_map/ppermute | solution.py:43
  89.6 23.3 %collective-permute-start.12 = (bf16[8,2,128,128]{3,2,1,0:T(8,128)(2,1)S(1)}, bf16[8,2,128,128]{3,2,1,0:T(8,128)(2,1)S(1)}, u32[]{:S(2)}, u32[]{:S(2)}) collective-permute-start(bf16[8,2,128,128]{3,2,1,0:T(8,128)(2,1)S(1)} %get-tuple-element.36), channel_id=1, source_target_pairs={{0,8},{8,16},{12,4},{16,24},{24,0},{28,20},{5,29},{9,17},{13,5},{2... | collective-permute-start | bytes 1572872 | tf_op jit(solution)/shard_map/ppermute | solution.py:43
  90.9 27.6 %collective-permute-start.8 = (bf16[8,2,128,128]{3,2,1,0:T(8,128)(2,1)S(1)}, bf16[8,2,128,128]{3,2,1,0:T(8,128)(2,1)S(1)}, u32[]{:S(2)}, u32[]{:S(2)}) collective-permute-start(bf16[8,2,128,128]{3,2,1,0:T(8,128)(2,1)S(1)} %copy-done.7), channel_id=1, source_target_pairs={{0,1},{4,5},{8,9},{12,13},{16,17},{20,21},{24,25},{28,29},{1,0},{5... | collective-permute-start | bytes 1572872 | tf_op jit(solution)/shard_map/ppermute | solution.py:43
  103.8 15.2 %collective-permute-start.9 = (bf16[8,2,128,128]{3,2,1,0:T(8,128)(2,1)}, bf16[8,2,128,128]{3,2,1,0:T(8,128)(2,1)S(1)}, u32[]{:S(2)}, u32[]{:S(2)}) collective-permute-start(bf16[8,2,128,128]{3,2,1,0:T(8,128)(2,1)} %get-tuple-element.33), channel_id=1, source_target_pairs={{8,9},{24,25},{13,12},{29,28},{10,11},{26,27},{15,14},{31,30}} | collective-permute-start | bytes 1572872 | tf_op jit(solution)/shard_map/ppermute | solution.py:43
  109.4 14.0 %collective-permute-start.22 = (bf16[8,2,128,128]{3,2,1,0:T(8,128)(2,1)}, bf16[8,2,128,128]{3,2,1,0:T(8,128)(2,1)S(1)}, u32[]{:S(2)}, u32[]{:S(2)}) collective-permute-start(bf16[8,2,128,128]{3,2,1,0:T(8,128)(2,1)} %get-tuple-element.48), channel_id=1, source_target_pairs={{0,1},{16,17},{5,4},{21,20},{2,3},{18,19},{7,6},{23,22}} | collective-permute-start | bytes 1572872 | tf_op jit(solution)/shard_map/ppermute | solution.py:43
  110.7 23.8 %collective-permute-start.21 = (bf16[8,2,128,128]{3,2,1,0:T(8,128)(2,1)}, bf16[8,2,128,128]{3,2,1,0:T(8,128)(2,1)}, u32[]{:S(2)}, u32[]{:S(2)}) collective-permute-start(bf16[8,2,128,128]{3,2,1,0:T(8,128)(2,1)} %get-tuple-element.47), channel_id=1, source_target_pairs={{0,1},{4,5},{8,9},{12,13},{16,17},{20,21},{24,25},{28,29},{1,0},{5... | collective-permute-start | bytes 1572872 | tf_op jit(solution)/shard_map/ppermute | solution.py:43
  112.9 21.6 %collective-permute-start.20 = (bf16[8,2,128,128]{3,2,1,0:T(8,128)(2,1)}, bf16[8,2,128,128]{3,2,1,0:T(8,128)(2,1)}, u32[]{:S(2)}, u32[]{:S(2)}) collective-permute-start(bf16[8,2,128,128]{3,2,1,0:T(8,128)(2,1)} %get-tuple-element.46), channel_id=1, source_target_pairs={{8,9},{24,25},{13,12},{29,28},{10,11},{26,27},{15,14},{31,30}} | collective-permute-start | bytes 1572872 | tf_op jit(solution)/shard_map/ppermute | solution.py:43
  118.6 23.5 %collective-permute-start.23 = (bf16[8,2,128,128]{3,2,1,0:T(8,128)(2,1)}, bf16[8,2,128,128]{3,2,1,0:T(8,128)(2,1)S(1)}, u32[]{:S(2)}, u32[]{:S(2)}) collective-permute-start(bf16[8,2,128,128]{3,2,1,0:T(8,128)(2,1)} %get-tuple-element.49), channel_id=1, source_target_pairs={{0,1},{4,5},{8,9},{12,13},{16,17},{20,21},{24,25},{28,29},{1,0},{5... | collective-permute-start | bytes 1572872 | tf_op jit(solution)/shard_map/ppermute | solution.py:43
  (1 other events, 0.8 us)
